TPU v7x, 32 devices: a whole 2x2x4 slice. The times are simulated.
32 devices in a mesh: dp: 8 (over z, x), seq: 4 (over y, core).
Axes of the slice: x: 2, y: 2, z: 4, core: 2. Of those that a mesh axis runs over, the one named last changes fastest.
Arguments:
- inputs: bfloat16 [4096, 1024], P(('dp', 'seq')), may hold values from -6 to 6
- gain_attn: bfloat16 [1024], P('dp'), may hold values from 0.25 to 1.75
- w_qkv: bfloat16 [1024, 3072], P('dp'), may hold values from -0.1875 to 0.1875
- b_qkv: bfloat16 [3072], P('dp'), may hold values from -5.5 to 5.5, as said below
- w_out: bfloat16 [1024, 1024], P('dp'), may hold values from -0.5 to 0.5
- gain_mlp: bfloat16 [1024], P('dp'), may hold values from 0.25 to 1.75
- w_gate: bfloat16 [1024, 2816], P('dp'), may hold values from -0.1875 to 0.1875
- w_up: bfloat16 [1024, 2816], P('dp'), may hold values from -0.1875 to 0.1875
- w_down: bfloat16 [2816, 1024], P('dp'), may hold values from -0.109375 to 0.109375
- cotangent: bfloat16 [4096, 1024], P(('dp', 'seq')), may hold values from -6 to 6
Outputs:
- output: bfloat16 [4096, 1024], P(('dp', 'seq'))
- grad_inputs: float32 [4096, 1024], P(('dp', 'seq'))
- grad_gain_attn: float32 [1024], P('dp')
- grad_w_qkv: float32 [1024, 3072], P('dp')
- grad_b_qkv: float32 [3072], P('dp')
- grad_w_out: float32 [1024, 1024], P('dp')
- grad_gain_mlp: float32 [1024], P('dp')
- grad_w_gate: float32 [1024, 2816], P('dp')
- grad_w_up: float32 [1024, 2816], P('dp')
- grad_w_down: float32 [2816, 1024], P('dp')
Inputs may be any that keep to these rules, and one draw needn't show every extreme that they name: `b_qkv`: entries of the joint projection's bias.
All inputs are finite; a program needn't handle non-finite values.
Results may differ from a plain program's by a relative error of at most 0.02.
The roundings to bfloat16 on the way count: a program that leaves them out, or rounds other values in their place, can miss the bound.
Values may be sent and summed in bfloat16 or wider, within the bound.
A program may use at most 192 MiB of HBM per device.

v0:
```python
import math

import jax
import jax.numpy as jnp
from jax import lax
from jax.sharding import PartitionSpec as P

HEADS = 16
KV_HEADS = 16
HEAD_DIM = 64


NORM_EPS = 1e-06
ROPE_BASE = 1000000.0
MASK_LOW = -1000000000.0


def rms_scale(signal, gain_vec):
    return (
        signal * lax.rsqrt(jnp.mean(signal * signal, axis=-1, keepdims=True) + NORM_EPS) * gain_vec
    )


def rotate(signal, cosine_tab, sine_tab):
    half_dim = signal.shape[-1] // 2
    turned = jnp.concatenate([-signal[..., half_dim:], signal[..., :half_dim]], axis=-1)
    return signal * cosine_tab + turned * sine_tab


def unrotate(grad_in, cosine_tab, sine_tab):
    half_dim = grad_in.shape[-1] // 2
    shifted = grad_in * sine_tab
    flipped = jnp.concatenate([shifted[..., half_dim:], -shifted[..., :half_dim]], axis=-1)
    return grad_in * cosine_tab + flipped


def rope_tables(positions):
    inverse_freq = 1.0 / ROPE_BASE ** (jnp.arange(0, HEAD_DIM, 2).astype(jnp.float32) / HEAD_DIM)
    angles = positions.astype(jnp.float32)[:, None] * inverse_freq[None, :]
    cosine_tab = jnp.cos(angles)
    sine_tab = jnp.sin(angles)
    return (
        jnp.concatenate([cosine_tab, cosine_tab], axis=-1),
        jnp.concatenate([sine_tab, sine_tab], axis=-1),
    )


def times_trans(left_op, weight):
    return lax.dot_general(
        left_op, weight, (((1,), (1,)), ((), ())), preferred_element_type=jnp.float32
    )


def trans_times(left_op, right_op):
    return lax.dot_general(
        left_op, right_op, (((0,), (0,)), ((), ())), preferred_element_type=jnp.float32
    )


def masked_scores(query_rows, keys_all, block_index, block_len):
    length = keys_all.shape[0]
    score_scale = 1.0 / math.sqrt(HEAD_DIM)
    scores = (
        jnp.einsum("qhe,khe->hqk", query_rows, keys_all, preferred_element_type=jnp.float32)
        * score_scale
    )
    query_pos = block_index * block_len + jnp.arange(block_len)
    key_pos = jnp.arange(length)
    return jnp.where(query_pos[:, None] >= key_pos[None, :], scores, MASK_LOW)


def attend_forward(queries, keys_all, values_all):
    length = queries.shape[0]
    block_len = min(512, length)
    block_count = length // block_len

    def one_block(block_index):
        scores = masked_scores(queries, keys_all, block_index, block_len)
        row_top = jnp.max(scores, axis=-1, keepdims=True)
        lifted = jnp.exp(scores - row_top)
        row_total = jnp.sum(lifted, axis=-1, keepdims=True)
        chances = (lifted / row_total).astype(jnp.bfloat16)
        block_out = jnp.einsum(
            "hqk,khe->qhe", chances, values_all, preferred_element_type=jnp.float32
        ).astype(jnp.bfloat16)
        log_total = (row_top + jnp.log(row_total))[..., 0]
        return (block_out, log_total)

    outs_all, log_totals = lax.map(one_block, jnp.arange(block_count))
    return (outs_all.reshape(queries.shape), log_totals)


def attend_backward(queries, keys_all, values_all, log_totals, grad_rows_all):
    length = queries.shape[0]
    block_len = min(512, length)
    block_count = length // block_len
    score_scale = 1.0 / math.sqrt(HEAD_DIM)

    def one_block(running, block_index):
        grad_keys, grad_values = running
        scores = masked_scores(queries, keys_all, block_index, block_len)
        log_total = lax.dynamic_index_in_dim(log_totals, block_index, 0, keepdims=False)
        chances = jnp.exp(scores - log_total[..., None])
        chances_low = chances.astype(jnp.bfloat16)
        grad_values = grad_values + jnp.einsum(
            "hqk,qhe->khe", chances_low, grad_rows_all, preferred_element_type=jnp.float32
        )
        grad_chances = jnp.einsum(
            "qhe,khe->hqk", grad_rows_all, values_all, preferred_element_type=jnp.float32
        )
        inner_sum = jnp.sum(chances * grad_chances, axis=-1, keepdims=True)
        grad_scores = (chances * (grad_chances - inner_sum)).astype(jnp.bfloat16)
        grad_query = (
            jnp.einsum("hqk,khe->qhe", grad_scores, keys_all, preferred_element_type=jnp.float32)
            * score_scale
        ).astype(jnp.bfloat16)
        grad_keys = (
            grad_keys
            + jnp.einsum("hqk,qhe->khe", grad_scores, queries, preferred_element_type=jnp.float32)
            * score_scale
        )
        return ((grad_keys, grad_values), grad_query)

    zeros_kv = jnp.zeros(keys_all.shape, jnp.float32)
    (grad_keys, grad_values), grad_queries = lax.scan(
        one_block, (zeros_kv, zeros_kv), jnp.arange(block_count)
    )
    return (
        grad_queries.reshape(queries.shape),
        grad_keys.astype(jnp.bfloat16),
        grad_values.astype(jnp.bfloat16),
    )


def body(inputs, gain_attn, w_qkv, b_qkv, w_out, gain_mlp, w_gate, w_up, w_down, cotangent):
    tokens = inputs.shape[0]
    repeat = HEADS // KV_HEADS
    q_width = HEADS * HEAD_DIM
    kv_width = KV_HEADS * HEAD_DIM
    ff_width = w_gate.shape[1]
    attn_set = (
        lax.all_gather(gain_attn, "dp", axis=0, tiled=True),
        lax.all_gather(w_qkv, "dp", axis=0, tiled=True),
        lax.all_gather(b_qkv, "dp", axis=0, tiled=True),
        lax.all_gather(w_out, "dp", axis=0, tiled=True),
    )
    mlp_set = (
        lax.all_gather(gain_mlp, "dp", axis=0, tiled=True),
        lax.all_gather(w_gate, "dp", axis=0, tiled=True),
        lax.all_gather(w_up, "dp", axis=0, tiled=True),
        lax.all_gather(w_down, "dp", axis=0, tiled=True),
    )
    gain_one, wqkv_full, bqkv_full, wout_full = attn_set
    gain_two, wgate_full, wup_full, wdown_full = mlp_set
    hidden_in = inputs.astype(jnp.float32)
    positions = lax.axis_index("seq") * tokens + jnp.arange(tokens, dtype=jnp.int32)
    cosine_tab, sine_tab = rope_tables(positions)
    cos_b = cosine_tab[:, None, :]
    sin_b = sine_tab[:, None, :]
    normed, norm_pull = jax.vjp(rms_scale, hidden_in, gain_one.astype(jnp.float32))
    normed_low = normed.astype(jnp.bfloat16)
    projected = jnp.dot(
        normed_low, wqkv_full, preferred_element_type=jnp.float32
    ) + bqkv_full.astype(jnp.float32)
    queries = projected[:, :q_width].reshape(tokens, HEADS, HEAD_DIM)
    keys_pre = projected[:, q_width : q_width + kv_width].reshape(tokens, KV_HEADS, HEAD_DIM)
    values_pre = projected[:, q_width + kv_width :].reshape(tokens, KV_HEADS, HEAD_DIM)
    queries_low = rotate(queries, cos_b, sin_b).astype(jnp.bfloat16)
    keys_low = jnp.repeat(rotate(keys_pre, cos_b, sin_b), repeat, axis=1).astype(jnp.bfloat16)
    values_low = jnp.repeat(values_pre, repeat, axis=1).astype(jnp.bfloat16)
    query_heads, key_heads, value_heads = (
        lax.all_to_all(queries_low, "seq", split_axis=1, concat_axis=0, tiled=True),
        lax.all_to_all(keys_low, "seq", split_axis=1, concat_axis=0, tiled=True),
        lax.all_to_all(values_low, "seq", split_axis=1, concat_axis=0, tiled=True),
    )
    attended, log_totals = attend_forward(query_heads, key_heads, value_heads)
    attended_tok = lax.all_to_all(attended, "seq", split_axis=0, concat_axis=1, tiled=True)
    attended_flat = attended_tok.reshape(tokens, q_width)
    middle = hidden_in + jnp.dot(attended_flat, wout_full, preferred_element_type=jnp.float32)
    normed_two, norm_two_pull = jax.vjp(rms_scale, middle, gain_two.astype(jnp.float32))
    normed_two_low = normed_two.astype(jnp.bfloat16)
    gate_pre = jnp.dot(normed_two_low, wgate_full, preferred_element_type=jnp.float32)
    up_proj = jnp.dot(normed_two_low, wup_full, preferred_element_type=jnp.float32)
    activated, act_pull = jax.vjp(
        lambda gate_in, up_in: jax.nn.silu(gate_in) * up_in, gate_pre, up_proj
    )
    activated_low = activated.astype(jnp.bfloat16)
    mlp_out = jnp.dot(activated_low, wdown_full, preferred_element_type=jnp.float32)
    output = (middle + mlp_out).astype(jnp.bfloat16)
    attn_back = (
        lax.all_gather(gain_attn, "dp", axis=0, tiled=True),
        lax.all_gather(w_qkv, "dp", axis=0, tiled=True),
        lax.all_gather(b_qkv, "dp", axis=0, tiled=True),
        lax.all_gather(w_out, "dp", axis=0, tiled=True),
    )
    mlp_back = (
        lax.all_gather(gain_mlp, "dp", axis=0, tiled=True),
        lax.all_gather(w_gate, "dp", axis=0, tiled=True),
        lax.all_gather(w_up, "dp", axis=0, tiled=True),
        lax.all_gather(w_down, "dp", axis=0, tiled=True),
    )
    wqkv_back = attn_back[1]
    wout_back = attn_back[3]
    wgate_back = mlp_back[1]
    wup_back = mlp_back[2]
    wdown_back = mlp_back[3]
    grad_out = cotangent.astype(jnp.float32)
    grad_act = times_trans(cotangent, wdown_back)
    grad_gate, grad_up = act_pull(grad_act)
    grad_gate_low = grad_gate.astype(jnp.bfloat16)
    grad_up_low = grad_up.astype(jnp.bfloat16)
    grad_normed_two = times_trans(grad_gate_low, wgate_back) + times_trans(grad_up_low, wup_back)
    grad_middle_norm, grad_gain_two = norm_two_pull(grad_normed_two)
    grad_middle = grad_out + grad_middle_norm
    grad_middle_low = grad_middle.astype(jnp.bfloat16)
    grad_attended = times_trans(grad_middle_low, wout_back).astype(jnp.bfloat16)
    grad_heads_in = lax.all_to_all(
        grad_attended.reshape(tokens, HEADS, HEAD_DIM),
        "seq",
        split_axis=1,
        concat_axis=0,
        tiled=True,
    )
    grad_q, grad_k, grad_v = attend_backward(
        query_heads, key_heads, value_heads, log_totals, grad_heads_in
    )
    grad_q_tok, grad_k_tok, grad_v_tok = (
        lax.all_to_all(grad_q, "seq", split_axis=0, concat_axis=1, tiled=True),
        lax.all_to_all(grad_k, "seq", split_axis=0, concat_axis=1, tiled=True),
        lax.all_to_all(grad_v, "seq", split_axis=0, concat_axis=1, tiled=True),
    )
    grad_k_sum = jnp.sum(
        grad_k_tok.astype(jnp.float32).reshape(tokens, KV_HEADS, repeat, HEAD_DIM), axis=2
    )
    grad_v_sum = jnp.sum(
        grad_v_tok.astype(jnp.float32).reshape(tokens, KV_HEADS, repeat, HEAD_DIM), axis=2
    )
    grad_q_pre = unrotate(grad_q_tok.astype(jnp.float32), cos_b, sin_b)
    grad_k_pre = unrotate(grad_k_sum, cos_b, sin_b)
    grad_proj = jnp.concatenate(
        [
            grad_q_pre.reshape(tokens, q_width),
            grad_k_pre.reshape(tokens, kv_width),
            grad_v_sum.reshape(tokens, kv_width),
        ],
        axis=1,
    ).astype(jnp.bfloat16)
    grad_normed = times_trans(grad_proj, wqkv_back)
    grad_hidden_norm, grad_gain_one = norm_pull(grad_normed)
    grad_inputs = grad_middle + grad_hidden_norm
    term_wqkv = trans_times(normed_low, grad_proj)
    term_bqkv = jnp.sum(grad_proj.astype(jnp.float32), axis=0)
    term_wout = trans_times(attended_flat, grad_middle_low)
    sum_gain_one, sum_wqkv, sum_bqkv, sum_wout, sum_gain_two = (
        lax.psum_scatter(
            grad_gain_one.astype(jnp.bfloat16), "dp", scatter_dimension=0, tiled=True
        ).astype(jnp.float32),
        lax.psum_scatter(
            term_wqkv.astype(jnp.bfloat16), "dp", scatter_dimension=0, tiled=True
        ).astype(jnp.float32),
        lax.psum_scatter(
            term_bqkv.astype(jnp.bfloat16), "dp", scatter_dimension=0, tiled=True
        ).astype(jnp.float32),
        lax.psum_scatter(
            term_wout.astype(jnp.bfloat16), "dp", scatter_dimension=0, tiled=True
        ).astype(jnp.float32),
        lax.psum_scatter(
            grad_gain_two.astype(jnp.bfloat16), "dp", scatter_dimension=0, tiled=True
        ).astype(jnp.float32),
    )
    gate_up_low = jnp.concatenate([grad_gate_low, grad_up_low], axis=1)
    columns = normed_two_low
    sum_gate_up = lax.psum_scatter(
        trans_times(columns, gate_up_low).astype(jnp.bfloat16),
        "dp",
        scatter_dimension=0,
        tiled=True,
    )
    columns = activated_low
    sum_down = lax.psum_scatter(
        trans_times(columns, cotangent).astype(jnp.bfloat16), "dp", scatter_dimension=0, tiled=True
    )
    totals = (
        lax.psum(sum_gain_one.astype(jnp.bfloat16), "seq").astype(jnp.float32),
        lax.psum(sum_wqkv.astype(jnp.bfloat16), "seq").astype(jnp.float32),
        lax.psum(sum_bqkv.astype(jnp.bfloat16), "seq").astype(jnp.float32),
        lax.psum(sum_wout.astype(jnp.bfloat16), "seq").astype(jnp.float32),
        lax.psum(sum_gain_two.astype(jnp.bfloat16), "seq").astype(jnp.float32),
        lax.psum(sum_gate_up, "seq").astype(jnp.float32),
        lax.psum(sum_down, "seq").astype(jnp.float32),
    )
    grad_gate_up = totals[5]
    return (
        output,
        grad_inputs,
        totals[0],
        totals[1],
        totals[2],
        totals[3],
        totals[4],
        grad_gate_up[:, :ff_width],
        grad_gate_up[:, ff_width:],
        totals[6],
    )


def solution(mesh):
    return jax.shard_map(
        body,
        mesh=mesh,
        in_specs=(
            P(("dp", "seq"), None),
            P("dp"),
            P("dp", None),
            P("dp"),
            P("dp", None),
            P("dp"),
            P("dp", None),
            P("dp", None),
            P("dp", None),
            P(("dp", "seq"), None),
        ),
        out_specs=(
            P(("dp", "seq"), None),
            P(("dp", "seq"), None),
            P("dp"),
            P("dp", None),
            P("dp"),
            P("dp", None),
            P("dp"),
            P("dp", None),
            P("dp", None),
            P("dp", None),
        ),
        check_vma=False,
    )
```

profile of v0, /device:TPU:0, one launch (start us, length us, event | category | flops | bytes accessed | tf_op | source)
XLA Modules:
  0.0 1037.4 jit_solution(9297631825862371351)
XLA Ops:
  10.6 22.6 %all-gather = bf16[8,1,128]{2,1,0:T(2,128)(2,1)S(1)} all-gather(bf16[1,1,128]{2,1,0:T(2,128)(2,1)S(1)} %bitcast.141), channel_id=1, replica_groups=mesh['dp'=8,'seq'=4] {'dp'}, dimensions={0}, use_global_device_ids=true | all-gather | bytes 2304 | tf_op jit(solution)/shard_map/all_gather | solution.py:142
  33.2 26.6 %all-gather.1 = bf16[8,1,384]{2,1,0:T(2,128)(2,1)S(1)} all-gather(bf16[1,1,384]{2,1,0:T(2,128)(2,1)S(1)} %reshape.163), channel_id=1, replica_groups=mesh['dp'=8,'seq'=4] {'dp'}, dimensions={0}, use_global_device_ids=true | all-gather | bytes 6912 | tf_op jit(solution)/shard_map/all_gather | solution.py:144
  60.1 51.7 %all-gather.9.cloned.1.call-done = bf16[1024,3072]{1,0:T(8,128)(2,1)} async-done(((bf16[128,3072]{1,0:T(8,128)(2,1)}), bf16[1024,3072]{1,0:T(8,128)(2,1)}) %all-gather.9.cloned.1.call-update) | async-done | bytes 6291472 | tf_op jit(solution)/shard_map/all_gather | solution.py:143
  111.8 3.8 convolution_add_fusion
  116.8 3.4 all-to-all-start
  121.5 4.7 all-to-all-done
  126.2 8.4 all_to_all.114
  134.6 3.4 all-to-all-start.1
  138.8 5.2 all-to-all-done.1
  145.9 1.4 copy-done
  148.5 1.1 reshape.173
  149.6 3.4 all-to-all-start.3
  153.0 18.0 %all-gather.2 = bf16[8,1,128]{2,1,0:T(2,128)(2,1)S(1)} all-gather(bf16[1,1,128]{2,1,0:T(2,128)(2,1)S(1)} %bitcast.142), channel_id=1, replica_groups=mesh['dp'=8,'seq'=4] {'dp'}, dimensions={0}, use_global_device_ids=true | all-gather | bytes 2304 | tf_op jit(solution)/shard_map/all_gather | solution.py:148
  171.7 2.1 multiply_reduce_fusion.3
  174.0 80.4 %all-gather.15.cloned.1.call-done = bf16[1024,2816]{1,0:T(8,128)(2,1)} async-done(((bf16[128,2816]{1,0:T(8,128)(2,1)}), bf16[1024,2816]{1,0:T(8,128)(2,1)}) %all-gather.15.cloned.1.call-update) | async-done | bytes 5767184 | tf_op jit(solution)/shard_map/all_gather | solution.py:150
  254.4 4.7 fusion.57
  259.0 87.9 %all-gather.13.cloned.1.call-done = bf16[1024,2816]{1,0:T(8,128)(2,1)} async-done(((bf16[128,2816]{1,0:T(8,128)(2,1)}), bf16[1024,2816]{1,0:T(8,128)(2,1)}) %all-gather.13.cloned.1.call-update) | async-done | bytes 5767184 | tf_op jit(solution)/shard_map/all_gather | solution.py:149
  346.9 4.7 fusion.56
  351.6 87.9 %all-gather.17.cloned.1.call-done = bf16[2816,1024]{1,0:T(8,128)(2,1)} async-done(((bf16[352,1024]{1,0:T(8,128)(2,1)}), bf16[2816,1024]{1,0:T(8,128)(2,1)}) %all-gather.17.cloned.1.call-update) | async-done | bytes 5767184 | tf_op jit(solution)/shard_map/all_gather | solution.py:151
  439.5 5.9 multiply_convert_fusion.1
  445.5 1.9 fusion.58
  447.4 4.7 multiply_reduce_fusion.1
  453.2 2.0 convolution_convert_fusion.3
  455.3 4.1 convolution_convert_fusion.1
  459.4 1.7 copy-done.4
  461.1 2.6 convolution_convert_fusion.4
  463.7 1.8 copy.98
  465.5 3.4 all-to-all-start.4
  468.9 6.0 all-to-all-done.4
  475.2 3.1 fusion.22
  478.6 1.1 reshape.175
  479.7 4.3 all-to-all-start.7
  484.0 3.4 multiply_reduce_fusion
  487.6 1.2 multiply_convert_fusion
  488.8 1.2 fusion.21
  489.9 2.0 copy.101
  492.0 2.1 reshape.179
  494.1 4.0 all-to-all-start.5
  498.1 1.5 fusion.20
  499.6 1.3 copy.106
  500.9 1.1 reshape.177
  502.0 2.2 all-to-all-done.5
  504.2 3.4 all-to-all-start.6
  507.7 1.3 reshape.176
  509.3 1.3 reshape.180
  511.2 2.4 all-to-all-done.6
  514.3 1.0 reshape.159
  515.2 1.1 copy.108
  516.8 4.5 convolution_convert_fusion.2
  521.4 1.0 copy-done.11
  522.6 5.9 convolution_convert_fusion
  528.9 106.3 %reduce-scatter.11.cloned.1.call-done = bf16[352,1024]{1,0:T(8,128)(2,1)} async-done(((bf16[2816,1024]{1,0:T(8,128)(2,1)}), bf16[352,1024]{1,0:T(8,128)(2,1)}) %reduce-scatter.11.cloned.1.call-update) | async-done | bytes 720912 | tf_op jit(solution)/shard_map/reduce_scatter | solution.py:280
  635.3 121.0 %reduce-scatter.5.cloned.1.call-done = bf16[128,3072]{1,0:T(8,128)(2,1)} async-done(((bf16[1024,3072]{1,0:T(8,128)(2,1)}), bf16[128,3072]{1,0:T(8,128)(2,1)}) %reduce-scatter.5.cloned.1.call-update) | async-done | bytes 786448 | tf_op jit(solution)/shard_map/reduce_scatter | solution.py:258
  756.2 195.7 %reduce-scatter.9.cloned.1.call-done = bf16[128,5632]{1,0:T(8,128)(2,1)} async-done(((bf16[1024,5632]{1,0:T(8,128)(2,1)}), bf16[128,5632]{1,0:T(8,128)(2,1)}) %reduce-scatter.9.cloned.1.call-update) | async-done | bytes 1441808 | tf_op jit(solution)/shard_map/reduce_scatter | solution.py:273
  953.9 4.3 fusion.13
  958.4 5.4 fusion.29
  963.9 34.9 %all-reduce.3 = (bf16[1024]{0:T(1024)(128)(2,1)S(1)}, bf16[3072]{0:T(1024)(128)(2,1)S(1)}, bf16[1024]{0:T(1024)(128)(2,1)S(1)}) all-reduce(bf16[1024]{0:T(1024)(128)(2,1)S(1)} %get-tuple-element.48, bf16[3072]{0:T(1024)(128)(2,1)S(1)} %fusion.49, bf16[1024]{0:T(1024)(128)(2,1)S(1)} %get-tuple-element.46), channel_id=2, replica_groups=mesh['dp'=8,'seq'=4] {'dp'}, use_global_device_ids=true, to_apply=%region_8.9.clone | all-reduce | flops 5120 | bytes 20480
  999.0 6.5 all-reduce.4
  1007.1 1.0 fusion.31
  1008.1 15.1 %all-reduce.8.cloned.1.call-done = (bf16[128,3072]{1,0:T(8,128)(2,1)}, bf16[128,1024]{1,0:T(8,128)(2,1)}, bf16[128,5632]{1,0:T(8,128)(2,1)}, bf16[352,1024]{1,0:T(8,128)(2,1)}) async-done(((bf16[128,3072]{1,0:T(8,128)(2,1)}, bf16[128,1024]{1,0:T(8,128)(2,1)}, bf16[128,5632]{1,0:T(8,128)(2,1)}, bf16[352,1024]{1,0:T(8,128)(2,1)}), (bf16[128,3072]{1,0:T(8,128)(2,1)}, bf16[128,1024]{1,0:T(8,128)(2,1)}, ...) | async-done | bytes 3211280 | tf_op jit(solution)/shard_map/psum | solution.py:285
  1023.2 1.9 convert_element_type.256
  1025.1 2.4 convert_element_type.253
  1027.6 1.3 convert_element_type.262
  1028.8 1.8 fusion.52
  (128 shorter events, 17.7 us)
Async XLA Ops:
  7.2 3.4 copy-start.20
  7.2 3.4 copy-start.21
  7.2 52.8 %copy-start.3 = (bf16[128,1024]{1,0:T(8,128)(2,1)S(1)}, bf16[128,1024]{1,0:T(8,128)(2,1)}, u32[]{:S(2)}) copy-start(bf16[128,1024]{1,0:T(8,128)(2,1)} %param.10) | copy-start | bytes 786436
  7.2 104.6 %all-gather.9.cloned.1.call-start = ((), (), s32[]{:S(2)}) async-start(), calls=%async_computation.12 | async-start | bytes 7077888 | tf_op jit(solution)/shard_map/all_gather | solution.py:143
  7.9 163.8 %all-gather.11.cloned.1.call-start = ((), (), s32[]{:S(2)}) async-start(), calls=%async_computation.13 | async-start | bytes 2359296 | tf_op jit(solution)/shard_map/all_gather | solution.py:145
  8.7 245.7 %all-gather.15.cloned.1.call-start = ((), (), s32[]{:S(2)}) async-start(), calls=%async_computation.15 | async-start | bytes 6488064 | tf_op jit(solution)/shard_map/all_gather | solution.py:150
  9.4 337.5 %all-gather.13.cloned.1.call-start = ((), (), s32[]{:S(2)}) async-start(), calls=%async_computation.14 | async-start | bytes 6488064 | tf_op jit(solution)/shard_map/all_gather | solution.py:149
  10.0 429.5 %all-gather.17.cloned.1.call-start = ((), (), s32[]{:S(2)}) async-start(), calls=%async_computation.16 | async-start | bytes 6488064 | tf_op jit(solution)/shard_map/all_gather | solution.py:151
  116.8 9.4 all-to-all-start
  134.6 9.4 all-to-all-start.1
  138.4 7.4 copy-start.17
  138.8 6.5 copy-start.14
  145.3 2.0 copy-start
  147.3 5.7 copy-start.22
  149.6 21.5 %all-to-all-start.3 = ((bf16[4,2,16384]{2,1,0:T(2,128)(2,1)}), bf16[4,2,16384]{2,1,0:T(2,128)(2,1)S(1)}, u32[]{:S(2)}, u32[]{:S(2)}) async-start(bf16[4,2,16384]{2,1,0:T(2,128)(2,1)} %reshape.173), calls=%async_computation.3 | async-start | bytes 524288 | tf_op jit(solution)/shard_map/all_to_all | solution.py:177
  153.0 375.9 %reduce-scatter.7.cloned.1.call-start = ((), (), s32[]{:S(2)}) async-start(), calls=%async_computation.18 | async-start | bytes 2359296 | tf_op jit(solution)/shard_map/reduce_scatter | solution.py:264
  259.0 180.5 %copy-start.16 = (bf16[128,1024]{1,0:T(8,128)(2,1)S(1)}, bf16[128,1024]{1,0:T(8,128)(2,1)}, u32[]{:S(2)}) copy-start(bf16[128,1024]{1,0:T(8,128)(2,1)} %param.19) | copy-start | bytes 786436
  439.5 6.0 copy-start.2
  445.4 2.0 copy-start.12
  445.4 2.0 copy-start.10
  445.4 9.8 copy-start.8
  452.4 0.8 copy-start.5
  455.2 180.0 %reduce-scatter.11.cloned.1.call-start = ((), (), s32[]{:S(2)}) async-start(), calls=%async_computation.20 | async-start | bytes 6488064 | tf_op jit(solution)/shard_map/reduce_scatter | solution.py:280
  459.4 1.7 copy-start.4
  465.5 9.4 all-to-all-start.4
  475.2 8.8 copy-start.18
  479.7 14.4 %all-to-all-start.7 = ((bf16[4,2,16384]{2,1,0:T(2,128)(2,1)}), bf16[4,2,16384]{2,1,0:T(2,128)(2,1)}, u32[]{:S(2)}, u32[]{:S(2)}) async-start(bf16[4,2,16384]{2,1,0:T(2,128)(2,1)} %reshape.175), calls=%async_computation.7 | async-start | bytes 524288 | tf_op jit(solution)/shard_map/all_to_all | solution.py:230
  484.0 3.6 copy-start.1
  487.6 1.2 copy-start.15
  494.1 10.1 all-to-all-start.5
  504.2 9.4 all-to-all-start.6
  507.6 248.6 %reduce-scatter.5.cloned.1.call-start = ((), (), s32[]{:S(2)}) async-start(), calls=%async_computation.17 | async-start | bytes 7077888 | tf_op jit(solution)/shard_map/reduce_scatter | solution.py:258
  521.3 1.1 copy-start.11
  521.3 1.3 copy-start.13
  521.3 430.6 %reduce-scatter.9.cloned.1.call-start = ((), (), s32[]{:S(2)}) async-start(), calls=%async_computation.19 | async-start | bytes 12976128 | tf_op jit(solution)/shard_map/reduce_scatter | solution.py:273
  528.6 423.4 %copy-start.23 = (u32[32]{0:T(128)S(1)}, u32[32]{0:T(128)}, u32[]{:S(2)}) copy-start(u32[32]{0:T(128)} %constant.82) | copy-start | bytes 388
  528.6 425.3 %copy-start.9 = (bf16[128,2816]{1,0:T(8,128)(2,1)S(1)}, bf16[128,2816]{1,0:T(8,128)(2,1)}, u32[]{:S(2)}) copy-start(bf16[128,2816]{1,0:T(8,128)(2,1)} %copy-done.8) | copy-start | bytes 2162692
  528.6 494.6 %all-reduce.8.cloned.1.call-start = ((), (), s32[]{:S(2)}) async-start(), calls=%async_computation.21 | async-start | bytes 6422528 | tf_op jit(solution)/shard_map/psum | solution.py:285
  958.4 48.7 %copy-start.6 = (f32[128,1024]{1,0:T(8,128)S(1)}, f32[128,1024]{1,0:T(8,128)}, u32[]{:S(2)}) copy-start(f32[128,1024]{1,0:T(8,128)} %copy-done.5) | copy-start | bytes 1572868
  1023.2 4.4 copy-start.19
  1023.2 5.6 copy-start.7
Sparse Core Ops, SparseCore 0:
  10.2 101.6 all-gather.8
  114.0 47.2 all-gather.10
  163.5 90.8 all-gather.14
  256.4 90.4 all-gather.12
  348.9 90.4 all-gather.16
  455.3 66.5 reduce-scatter.6
  525.6 109.6 reduce-scatter.10
  638.8 117.3 reduce-scatter.4
  759.8 192.0 reduce-scatter.8
  954.4 68.7 all-reduce.7
where the time goes:
time: 1040 us
  waiting for transfers between devices  770 us (74%)
  blocking collectives  117 us (11%)
  matrix products  67.6 us (6%)
  local copies, waits for them, and re-layouts  28.5 us (3%)
  starting transfers between devices  26 us (2%)
  between operations  16.2 us (2%)
  other arithmetic  12.5 us (1%)
    reduce_scatter x1, waiting for transfers between devices, body(): lax.psum_scatter(trans_times(columns, gate_up_low).astype(jnp.bfloat16),...  196 us
    reduce_scatter x1, waiting for transfers between devices, body(): lax.psum_scatter(term_wqkv.astype(jnp.bfloat16), 'dp', scatter_dimension=...  121 us
    reduce_scatter x1, waiting for transfers between devices, body(): lax.psum_scatter(trans_times(columns, cotangent).astype(jnp.bfloat16), 'd...  106 us
    all_gather x1, waiting for transfers between devices, body(): lax.all_gather(w_gate, 'dp', axis=0, tiled=True)  87.9 us
    all_gather x1, waiting for transfers between devices, body(): lax.all_gather(w_down, 'dp', axis=0, tiled=True)  87.9 us
    all_gather x1, waiting for transfers between devices, body(): lax.all_gather(w_up, 'dp', axis=0, tiled=True)  80.4 us
    all_gather x1, waiting for transfers between devices, body(): lax.all_gather(w_qkv, 'dp', axis=0, tiled=True)  51.7 us
    unnamed x1, blocking collectives  34.9 us
  transfers between devices with their start and end apart: 17, of which 13 were waited for; matrix products, arithmetic and copies ran while one was open for 8% of the time, Pallas kernels for 0%

commit v1 on v0

--- a/solution.py
+++ b/solution.py
@@ -3,6 +3,8 @@
 import jax
 import jax.numpy as jnp
 from jax import lax
+from jax.experimental import pallas as pl
+from jax.experimental.pallas import tpu as pltpu
 from jax.sharding import PartitionSpec as P
 
 HEADS = 16
@@ -132,7 +134,7 @@
     )
 
 
-def body(inputs, gain_attn, w_qkv, b_qkv, w_out, gain_mlp, w_gate, w_up, w_down, cotangent):
+def generic_body(inputs, gain_attn, w_qkv, b_qkv, w_out, gain_mlp, w_gate, w_up, w_down, cotangent):
     tokens = inputs.shape[0]
     repeat = HEADS // KV_HEADS
     q_width = HEADS * HEAD_DIM
@@ -304,9 +306,855 @@
     )
 
 
+Z_LEN = 4
+X_LEN = 2
+SEQ_PARTS = 4
+MESH = pl.DeviceIdType.MESH
+HBM = pl.BlockSpec(memory_space=pl.ANY)
+VMEM = pl.BlockSpec(memory_space=pltpu.VMEM)
+BF16 = jnp.bfloat16
+F32 = jnp.float32
+
+
+def place():
+    dp = lax.axis_index("dp")
+    part = lax.axis_index("seq")
+    z, x = lax.div(dp, X_LEN), lax.rem(dp, X_LEN)
+    return dp, part, z, x
+
+
+def quarter_of(part):
+    y, core = lax.div(part, 2), lax.rem(part, 2)
+    return (1 - y) * 3 * core + y * (1 + core)
+
+
+def turn(value, step, length):
+    return lax.rem(value + step, length)
+
+
+def remote(source, target, send, recv, dp, part):
+    return pltpu.make_async_remote_copy(
+        src_ref=source,
+        dst_ref=target,
+        send_sem=send,
+        recv_sem=recv,
+        device_id=(dp, part),
+        device_id_type=MESH,
+    )
+
+
+def block(index, size):
+    return pl.ds(pl.multiple_of(index * size, size), size)
+
+
+def greet(partners):
+    barrier = pltpu.get_barrier_semaphore()
+    for dp, part in partners:
+        pl.semaphore_signal(barrier, inc=1, device_id=(dp, part), device_id_type=MESH)
+    pl.semaphore_wait(barrier, len(partners))
+
+
+def z_partners(dp, part, z, x):
+    return [(turn(z, step, Z_LEN) * X_LEN + x, part) for step in range(1, Z_LEN)]
+
+
+def seq_partners(dp, part):
+    return [(dp, turn(part, step, SEQ_PARTS)) for step in range(1, SEQ_PARTS)]
+
+
+class ColumnGather:
+    def __init__(self, source, dest, send, recv, local, base):
+        self.source, self.dest, self.send, self.recv, self.local, self.base = (
+            source, dest, send, recv, local, base,
+        )
+        self.rows = dest.shape[0] // (Z_LEN * X_LEN)
+
+    def slot(self, dp):
+        return self.dest.at[block(dp, self.rows)]
+
+    def copy(self, source, slot, index, dp, part):
+        return remote(
+            source, slot, self.send.at[self.base + index], self.recv.at[self.base + index], dp, part
+        )
+
+    def start(self):
+        dp, part, z, x = place()
+        mine = self.slot(dp)
+        self.own = pltpu.make_async_copy(self.source, mine, self.local)
+        self.own.start()
+        self.sent = []
+        for step in range(1, Z_LEN):
+            self.sent.append(
+                self.copy(self.source, mine, step - 1, turn(z, step, Z_LEN) * X_LEN + x, part)
+            )
+        self.sent.append(self.copy(self.source, mine, 3, z * X_LEN + 1 - x, part))
+        for each in self.sent:
+            each.start()
+
+    def relay(self):
+        dp, part, z, x = place()
+        for step in range(1, Z_LEN):
+            slot = self.slot(turn(z, Z_LEN - step, Z_LEN) * X_LEN + x)
+            self.copy(slot, slot, step - 1, dp, part).wait_recv()
+            onward = self.copy(slot, slot, 3 + step, z * X_LEN + 1 - x, part)
+            onward.start()
+            self.sent.append(onward)
+
+    def arrive(self):
+        dp, part, z, x = place()
+        self.own.wait()
+        for step in range(Z_LEN):
+            slot = self.slot(turn(z, Z_LEN - step, Z_LEN) * X_LEN + 1 - x)
+            self.copy(slot, slot, 3 + step, dp, part).wait_recv()
+
+    def drain(self):
+        for each in self.sent:
+            each.wait_send()
+
+
+class RowGather:
+    def __init__(self, source, dest, send, recv, local, base):
+        self.source, self.dest, self.send, self.recv, self.local, self.base = (
+            source, dest, send, recv, local, base,
+        )
+        self.rows = dest.shape[0] // X_LEN
+
+    def slot(self, x):
+        return self.dest.at[block(x, self.rows)]
+
+    def copy(self, source, slot, send, recv, dp, part):
+        return remote(
+            source, slot, self.send.at[self.base + send], self.recv.at[self.base + recv], dp, part
+        )
+
+    def start(self):
+        dp, part, z, x = place()
+        quarter = quarter_of(part)
+        mine = self.slot(x)
+
+        @pl.when(z == quarter)
+        def _():
+            pltpu.make_async_copy(self.source, mine, self.local).start()
+            for step in range(1, Z_LEN):
+                self.copy(
+                    self.source, mine, step - 1, 0, turn(z, step, Z_LEN) * X_LEN + x, part
+                ).start()
+            self.copy(self.source, mine, 3, 1, z * X_LEN + 1 - x, part).start()
+
+    def relay(self):
+        dp, part, z, x = place()
+        mine = self.slot(x)
+
+        @pl.when(z != quarter_of(part))
+        def _():
+            self.copy(mine, mine, 0, 0, dp, part).wait_recv()
+            self.copy(mine, mine, 3, 1, z * X_LEN + 1 - x, part).start()
+
+    def arrive(self):
+        dp, part, z, x = place()
+        mine, other = self.slot(x), self.slot(1 - x)
+
+        @pl.when(z == quarter_of(part))
+        def _():
+            pltpu.make_async_copy(self.source, mine, self.local).wait()
+
+        self.copy(other, other, 3, 1, dp, part).wait_recv()
+
+    def drain(self):
+        dp, part, z, x = place()
+        mine = self.slot(x)
+
+        @pl.when(z == quarter_of(part))
+        def _():
+            for step in range(1, Z_LEN):
+                self.copy(self.source, mine, step - 1, 0, dp, part).wait_send()
+
+        self.copy(self.source, mine, 3, 1, dp, part).wait_send()
+
+
+class SeqGather:
+    def __init__(self, source, dest, send, recv, local, base):
+        self.source, self.dest, self.send, self.recv, self.local, self.base = (
+            source, dest, send, recv, local, base,
+        )
+        self.rows = dest.shape[0] // SEQ_PARTS
+
+    def copy(self, slot, index, dp, part):
+        return remote(
+            self.source,
+            self.dest.at[block(slot, self.rows)],
+            self.send.at[self.base + index],
+            self.recv.at[self.base + index],
+            dp,
+            part,
+        )
+
+    def start(self):
+        dp, part, z, x = place()
+        self.own = pltpu.make_async_copy(
+            self.source, self.dest.at[block(part, self.rows)], self.local
+        )
+        self.own.start()
+        for step in range(1, SEQ_PARTS):
+            self.copy(part, step - 1, dp, turn(part, step, SEQ_PARTS)).start()
+
+    def arrive(self):
+        dp, part, z, x = place()
+        self.own.wait()
+        for step in range(1, SEQ_PARTS):
+            self.copy(turn(part, SEQ_PARTS - step, SEQ_PARTS), step - 1, dp, part).wait_recv()
+
+    def drain(self):
+        dp, part, z, x = place()
+        for step in range(1, SEQ_PARTS):
+            self.copy(part, step - 1, dp, part).wait_send()
+
+
+def gather_kernel(
+    x_in, cot, small, qkv, wout, gate_up, wdown,
+    x_all, cot_all, small_all, qkv_all, wout_all, gate_up_all, wdown_all,
+    send, recv, local,
+):
+    dp, part, z, x = place()
+    greet(
+        z_partners(dp, part, z, x)
+        + [(z * X_LEN + 1 - x, part)]
+        + seq_partners(dp, part)
+    )
+    seq_moves = [
+        SeqGather(x_in, x_all, send, recv, local.at[0], 0),
+        SeqGather(cot, cot_all, send, recv, local.at[1], 3),
+    ]
+    moves = [
+        ColumnGather(small, small_all, send, recv, local.at[2], 8),
+        ColumnGather(qkv, qkv_all, send, recv, local.at[3], 16),
+        RowGather(wout, wout_all, send, recv, local.at[4], 24),
+        ColumnGather(gate_up, gate_up_all, send, recv, local.at[5], 32),
+        RowGather(wdown, wdown_all, send, recv, local.at[6], 40),
+    ]
+    for move in seq_moves + moves:
+        move.start()
+    for move in moves:
+        move.relay()
+    for move in seq_moves + moves:
+        move.arrive()
+    for move in seq_moves + moves:
+        move.drain()
+
+
+def gather_all(x_in, cot, small, qkv, wout, gate_up, wdown):
+    def grown(array, times):
+        return jax.ShapeDtypeStruct((array.shape[0] * times,) + array.shape[1:], array.dtype)
+
+    dp = Z_LEN * X_LEN
+    return pl.pallas_call(
+        gather_kernel,
+        out_shape=(
+            grown(x_in, SEQ_PARTS), grown(cot, SEQ_PARTS), grown(small, dp), grown(qkv, dp),
+            grown(wout, X_LEN), grown(gate_up, dp), grown(wdown, X_LEN),
+        ),
+        in_specs=[HBM] * 7,
+        out_specs=[VMEM] * 7,
+        scratch_shapes=[
+            pltpu.SemaphoreType.DMA((48,)),
+            pltpu.SemaphoreType.DMA((48,)),
+            pltpu.SemaphoreType.DMA((8,)),
+        ],
+        compiler_params=pltpu.CompilerParams(collective_id=0, has_side_effects=True),
+    )(x_in, cot, small, qkv, wout, gate_up, wdown)
+
+
+def over_rows(count, step, work):
+    def one(index, carry):
+        work(pl.ds(pl.multiple_of(index * step, step), step))
+        return carry
+
+    lax.fori_loop(0, count // step, one, 0)
+
+
+def mean_square(value):
+    return lax.rsqrt(jnp.mean(value * value, axis=-1, keepdims=True) + NORM_EPS)
+
+
+class SeqReduce:
+    def __init__(self, partial, outbox, inbox, send, recv, base):
+        self.partial, self.outbox, self.inbox, self.send, self.recv, self.base = (
+            partial, outbox, inbox, send, recv, base,
+        )
+        self.rows = partial.shape[0] // SEQ_PARTS
+
+    def copy(self, index, dp, part):
+        return remote(
+            self.outbox.at[index],
+            self.inbox.at[index],
+            self.send.at[self.base + index],
+            self.recv.at[self.base + index],
+            dp,
+            part,
+        )
+
+    def start(self):
+        dp, part, z, x = place()
+        for step in range(1, SEQ_PARTS):
+            target = turn(part, step, SEQ_PARTS)
+
+            def work(rows, target=target, step=step):
+                self.outbox[step - 1, rows, :] = self.partial[
+                    pl.ds(pl.multiple_of(target * self.rows + rows.start, rows.size), rows.size), :
+                ].astype(BF16)
+
+            over_rows(self.rows, 16, work)
+            self.copy(step - 1, dp, target).start()
+
+    def arrive(self):
+        dp, part, z, x = place()
+        for step in range(1, SEQ_PARTS):
+            self.copy(step - 1, dp, part).wait_recv()
+
+    def total(self, rows):
+        dp, part, z, x = place()
+        value = self.partial[
+            pl.ds(pl.multiple_of(part * self.rows + rows.start, rows.size), rows.size), :
+        ]
+        for step in range(SEQ_PARTS - 1):
+            value = value + self.inbox[step, rows, :].astype(F32)
+        return value
+
+    def drain(self):
+        dp, part, z, x = place()
+        for step in range(1, SEQ_PARTS):
+            self.copy(step - 1, dp, part).wait_send()
+
+
+def middle_kernel(partial, x_in, gain, mid, normed_all, normed, outbox, inbox, send, recv, local):
+    dp, part, z, x = place()
+    greet(seq_partners(dp, part))
+    reduce = SeqReduce(partial, outbox, inbox, send, recv, 0)
+    reduce.start()
+    reduce.arrive()
+
+    def work(rows):
+        value = x_in[rows, :].astype(F32) + reduce.total(rows)
+        mid[rows, :] = value
+        normed[rows, :] = (value * mean_square(value) * gain[...]).astype(BF16)
+
+    over_rows(x_in.shape[0], 16, work)
+    spread = SeqGather(normed, normed_all, send, recv, local.at[0], 3)
+    spread.start()
+    spread.arrive()
+    reduce.drain()
+    spread.drain()
+
+
+def seq_scratch(rows, width):
+    return [
+        pltpu.VMEM((rows, width), BF16),
+        pltpu.VMEM((SEQ_PARTS - 1, rows, width), BF16),
+        pltpu.VMEM((SEQ_PARTS - 1, rows, width), BF16),
+        pltpu.SemaphoreType.DMA((8,)),
+        pltpu.SemaphoreType.DMA((8,)),
+        pltpu.SemaphoreType.DMA((1,)),
+    ]
+
+
+def middle_step(partial, x_in, gain):
+    rows, width = x_in.shape
+    return pl.pallas_call(
+        middle_kernel,
+        out_shape=(
+            jax.ShapeDtypeStruct((rows, width), F32),
+            jax.ShapeDtypeStruct((rows * SEQ_PARTS, width), BF16),
+        ),
+        in_specs=[VMEM] * 3,
+        out_specs=[VMEM] * 2,
+        scratch_shapes=seq_scratch(rows, width),
+        compiler_params=pltpu.CompilerParams(collective_id=1, has_side_effects=True),
+    )(partial, x_in, gain)
+
+
+def rms_back(value, grad, gain):
+    scale = mean_square(value)
+    unit = value * scale
+    pulled = grad * gain
+    inner = jnp.mean(pulled * unit, axis=-1, keepdims=True)
+    return scale * (pulled - unit * inner), grad * unit
+
+
+def back_kernel(
+    partial, mid, base, gain, grad_mid, low_all, grad_gain, low, outbox, inbox, send, recv, local
+):
+    dp, part, z, x = place()
+    greet(seq_partners(dp, part))
+    reduce = SeqReduce(partial, outbox, inbox, send, recv, 0)
+    reduce.start()
+    grad_gain[...] = jnp.zeros_like(grad_gain)
+    reduce.arrive()
+
+    def work(rows):
+        pulled, summand = rms_back(mid[rows, :], reduce.total(rows), gain[...])
+        total = base[rows, :].astype(F32) + pulled
+        grad_mid[rows, :] = total
+        low[rows, :] = total.astype(BF16)
+        grad_gain[...] += jnp.sum(summand, axis=0, keepdims=True)
+
+    over_rows(mid.shape[0], 16, work)
+    spread = SeqGather(low, low_all, send, recv, local.at[0], 3)
+    spread.start()
+    spread.arrive()
+    reduce.drain()
+    spread.drain()
+
+
+def back_step(partial, mid, base, gain, number):
+    rows, width = mid.shape
+    return pl.pallas_call(
+        back_kernel,
+        out_shape=(
+            jax.ShapeDtypeStruct((rows, width), F32),
+            jax.ShapeDtypeStruct((rows * SEQ_PARTS, width), BF16),
+            jax.ShapeDtypeStruct((1, width), F32),
+        ),
+        in_specs=[VMEM] * 4,
+        out_specs=[VMEM] * 3,
+        scratch_shapes=seq_scratch(rows, width),
+        compiler_params=pltpu.CompilerParams(collective_id=number, has_side_effects=True),
+    )(partial, mid, base, gain)
+
+
+class ColumnReduce:
+    def __init__(self, grads, xbox, hold, zbox, out, send, recv, base):
+        self.grads, self.xbox, self.hold, self.zbox, self.out = grads, xbox, hold, zbox, out
+        self.send, self.recv, self.base = send, recv, base
+        self.rows = grads.shape[0] // (Z_LEN * X_LEN)
+
+    def copy(self, source, slot, index, dp, part):
+        return remote(
+            source, slot, self.send.at[self.base + index], self.recv.at[self.base + index], dp, part
+        )
+
+    def order(self):
+        return range(Z_LEN - 1, -1, -1)
+
+    def cross(self, step):
+        dp, part, z, x = place()
+        target = turn(z, step, Z_LEN)
+        return self.copy(
+            self.grads.at[block(target * X_LEN + 1 - x, self.rows)],
+            self.xbox.at[step],
+            step,
+            z * X_LEN + 1 - x,
+            part,
+        )
+
+    def along(self, step):
+        dp, part, z, x = place()
+        return self.copy(
+            self.hold.at[step],
+            self.zbox.at[step],
+            3 + step,
+            turn(z, step, Z_LEN) * X_LEN + x,
+            part,
+        )
+
+    def share(self, step):
+        dp, part, z, x = place()
+        return self.copy(
+            self.out.at[part], self.out.at[part], 6 + step, dp, turn(part, step, SEQ_PARTS)
+        )
+
+    def start(self):
+        for step in self.order():
+            self.cross(step).start()
+
+    def relay(self):
+        dp, part, z, x = place()
+        for step in self.order():
+            self.cross(step).wait_recv()
+            mine = turn(z, step, Z_LEN) * X_LEN + x
+
+            def work(rows, step=step, mine=mine):
+                here = pl.ds(pl.multiple_of(mine * self.rows + rows.start, 16), 16)
+                self.hold[step, rows, :] = (
+                    self.grads[here, :].astype(F32) + self.xbox[step, rows, :].astype(F32)
+                ).astype(BF16)
+
+            over_rows(self.rows, 16, work)
+            if step:
+                self.along(step).start()
+
+    def finish(self):
+        dp, part, z, x = place()
+        for step in range(1, Z_LEN):
+            self.along(step).wait_recv()
+
+        def work(rows):
+            value = self.hold[0, rows, :].astype(F32)
+            for step in range(1, Z_LEN):
+                value = value + self.zbox[step, rows, :].astype(F32)
+            self.out[part, rows, :] = value.astype(BF16)
+
+        over_rows(self.rows, 16, work)
+        for step in range(1, SEQ_PARTS):
+            self.share(step).start()
+
+    def drain(self):
+        dp, part, z, x = place()
+        for step in range(1, SEQ_PARTS):
+            slot = self.out.at[turn(part, SEQ_PARTS - step, SEQ_PARTS)]
+            self.copy(slot, slot, 6 + step, dp, part).wait_recv()
+            self.share(step).wait_send()
+            self.along(step).wait_send()
+        for step in self.order():
+            self.cross(step).wait_send()
+
+
+class RowReduce:
+    def __init__(self, grads, xbox, hold, zbox, out, send, recv, base):
+        self.grads, self.xbox, self.hold, self.zbox, self.out = grads, xbox, hold, zbox, out
+        self.send, self.recv, self.base = send, recv, base
+        self.rows = grads.shape[0] // X_LEN
+
+    def copy(self, source, slot, send, recv, dp, part):
+        return remote(
+            source, slot, self.send.at[self.base + send], self.recv.at[self.base + recv], dp, part
+        )
+
+    def cross(self):
+        dp, part, z, x = place()
+        return self.copy(
+            self.grads.at[block(1 - x, self.rows)], self.xbox, 0, 0, z * X_LEN + 1 - x, part
+        )
+
+    def along(self, step):
+        dp, part, z, x = place()
+        return self.copy(
+            self.hold, self.zbox.at[step], 1, 1 + step, quarter_of(part) * X_LEN + x, part
+        )
+
+    def share(self, step, source_part):
+        dp, part, z, x = place()
+        return self.copy(
+            self.out, self.out, 1 + step, 5, dp, turn(source_part, step, SEQ_PARTS)
+        )
+
+    def start(self):
+        self.cross().start()
+
+    def relay(self):
+        dp, part, z, x = place()
+        self.cross().wait_recv()
+
+        def work(rows):
+            here = pl.ds(pl.multiple_of(x * self.rows + rows.start, 16), 16)
+            self.hold[rows, :] = (
+                self.grads[here, :].astype(F32) + self.xbox[rows, :].astype(F32)
+            ).astype(BF16)
+
+        over_rows(self.rows, 16, work)
+        gap = turn(quarter_of(part), Z_LEN - z, Z_LEN)
+        for step in range(1, Z_LEN):
+
+            @pl.when(gap == step)
+            def _(step=step):
+                self.along(step).start()
+
+    def finish(self):
+        dp, part, z, x = place()
+
+        @pl.when(z == quarter_of(part))
+        def _():
+            for step in range(1, Z_LEN):
+                self.along(step).wait_recv()
+
+            def work(rows):
+                value = self.hold[rows, :].astype(F32)
+                for step in range(1, Z_LEN):
+                    value = value + self.zbox[step, rows, :].astype(F32)
+                self.out[rows, :] = value.astype(BF16)
+
+            over_rows(self.rows, 16, work)
+            for step in range(1, SEQ_PARTS):
+                self.share(step, part).start()
+
+    def drain(self):
+        dp, part, z, x = place()
+        self.cross().wait_send()
+
+        @pl.when(z == quarter_of(part))
+        def _():
+            for step in range(1, SEQ_PARTS):
+                self.share(step, part).wait_send()
+
+        @pl.when(z != quarter_of(part))
+        def _():
+            self.along(1).wait_send()
+            self.copy(self.out, self.out, 1, 5, dp, part).wait_recv()
+
+
+class VectorReduce:
+    def __init__(self, vector, seq_box, dp_box, out, send, recv, base):
+        self.vector, self.seq_box, self.dp_box, self.out = vector, seq_box, dp_box, out
+        self.send, self.recv, self.base = send, recv, base
+        self.rows = vector.shape[0] // (Z_LEN * X_LEN)
+
+    def copy(self, source, slot, index, dp, part):
+        return remote(
+            source, slot, self.send.at[self.base + index], self.recv.at[self.base + index], dp, part
+        )
+
+    def near(self, step):
+        dp, part, z, x = place()
+        return self.copy(
+            self.seq_box.at[part], self.seq_box.at[part], step, dp, turn(part, step, SEQ_PARTS)
+        )
+
+    def far(self, step):
+        dp, part, z, x = place()
+        target = turn(dp, step, Z_LEN * X_LEN)
+        return self.copy(
+            self.vector.at[block(target, self.rows)], self.dp_box.at[dp], 4 + step, target, part
+        )
+
+    def start(self):
+        dp, part, z, x = place()
+        self.seq_box[part] = self.vector[...]
+        for step in range(1, SEQ_PARTS):
+            self.near(step).start()
+
+    def relay(self):
+        dp, part, z, x = place()
+        for step in range(1, SEQ_PARTS):
+            slot = self.seq_box.at[turn(part, SEQ_PARTS - step, SEQ_PARTS)]
+            self.copy(slot, slot, step, dp, part).wait_recv()
+        value = self.seq_box[0]
+        for step in range(1, SEQ_PARTS):
+            value = value + self.seq_box[step]
+        self.vector[...] = value
+        self.dp_box[dp] = self.vector[block(dp, self.rows), :]
+        for step in range(1, Z_LEN * X_LEN):
+            self.far(step).start()
+
+    def finish(self):
+        dp, part, z, x = place()
+        count = Z_LEN * X_LEN
+        for step in range(1, count):
+            slot = self.dp_box.at[turn(dp, count - step, count)]
+            self.copy(slot, slot, 4 + step, dp, part).wait_recv()
+        value = self.dp_box[0]
+        for step in range(1, count):
+            value = value + self.dp_box[step]
+        self.out[...] = value
+
+    def drain(self):
+        for step in range(1, SEQ_PARTS):
+            self.near(step).wait_send()
+        for step in range(1, Z_LEN * X_LEN):
+            self.far(step).wait_send()
+
+
+def reduce_kernel(
+    vector_in, down, gate_up, wout, qkv,
+    vector_out, down_out, gate_up_out, wout_out, qkv_out,
+    vector, seq_box, dp_box,
+    down_x, down_h, down_z, gu_x, gu_h, gu_z, wout_x, wout_h, wout_z, qkv_x, qkv_h, qkv_z,
+    send, recv,
+):
+    dp, part, z, x = place()
+    greet(
+        [(turn(dp, step, Z_LEN * X_LEN), part) for step in range(1, Z_LEN * X_LEN)]
+        + seq_partners(dp, part)
+    )
+    vector[...] = vector_in[...]
+    moves = [
+        VectorReduce(vector, seq_box, dp_box, vector_out, send, recv, 0),
+        RowReduce(down, down_x, down_h, down_z, down_out, send, recv, 16),
+        ColumnReduce(gate_up, gu_x, gu_h, gu_z, gate_up_out, send, recv, 24),
+        RowReduce(wout, wout_x, wout_h, wout_z, wout_out, send, recv, 36),
+        ColumnReduce(qkv, qkv_x, qkv_h, qkv_z, qkv_out, send, recv, 44),
+    ]
+    for move in moves:
+        move.start()
+    for move in moves:
+        move.relay()
+    for move in moves:
+        move.finish()
+    for move in moves:
+        move.drain()
+
+
+def reduce_all(vector, down, gate_up, wout, qkv):
+    def row_boxes(array):
+        rows, width = array.shape[0] // X_LEN, array.shape[1]
+        return [
+            pltpu.VMEM((rows, width), BF16),
+            pltpu.VMEM((rows, width), BF16),
+            pltpu.VMEM((Z_LEN, rows, width), BF16),
+        ]
+
+    def column_boxes(array):
+        rows, width = array.shape[0] // (Z_LEN * X_LEN), array.shape[1]
+        return [pltpu.VMEM((Z_LEN, rows, width), BF16)] * 3
+
+    count = Z_LEN * X_LEN
+    return pl.pallas_call(
+        reduce_kernel,
+        out_shape=(
+            jax.ShapeDtypeStruct((vector.shape[0] // count, vector.shape[1]), F32),
+            jax.ShapeDtypeStruct((down.shape[0] // X_LEN, down.shape[1]), BF16),
+            jax.ShapeDtypeStruct((SEQ_PARTS, gate_up.shape[0] // count, gate_up.shape[1]), BF16),
+            jax.ShapeDtypeStruct((wout.shape[0] // X_LEN, wout.shape[1]), BF16),
+            jax.ShapeDtypeStruct((SEQ_PARTS, qkv.shape[0] // count, qkv.shape[1]), BF16),
+        ),
+        in_specs=[VMEM] * 5,
+        out_specs=[VMEM] * 5,
+        scratch_shapes=[
+            pltpu.VMEM(vector.shape, F32),
+            pltpu.VMEM((SEQ_PARTS,) + vector.shape, F32),
+            pltpu.VMEM((count, vector.shape[0] // count, vector.shape[1]), F32),
+        ]
+        + row_boxes(down)
+        + column_boxes(gate_up)
+        + row_boxes(wout)
+        + column_boxes(qkv)
+        + [pltpu.SemaphoreType.DMA((56,)), pltpu.SemaphoreType.DMA((56,))],
+        compiler_params=pltpu.CompilerParams(collective_id=4, has_side_effects=True),
+    )(vector, down, gate_up, wout, qkv)
+
+
+def ring_body(inputs, gain_attn, w_qkv, b_qkv, w_out, gain_mlp, w_gate, w_up, w_down, cotangent):
+    rows, width = inputs.shape
+    count = Z_LEN * X_LEN
+    part = lax.axis_index("seq")
+    dp = lax.axis_index("dp")
+    quarter = quarter_of(part)
+    heads = HEADS // SEQ_PARTS
+    inner = heads * HEAD_DIM
+    ff_part = w_gate.shape[1] // SEQ_PARTS
+    whole = ff_part // 128 * 128
+    tokens = rows * SEQ_PARTS
+
+    qkv_mine = lax.dynamic_index_in_dim(
+        w_qkv.reshape(w_qkv.shape[0], 3, SEQ_PARTS, inner), quarter, 2, keepdims=False
+    ).reshape(w_qkv.shape[0], 3 * inner)
+    gate_mine = lax.dynamic_slice_in_dim(w_gate, quarter * ff_part, ff_part, 1)
+    up_mine = lax.dynamic_slice_in_dim(w_up, quarter * ff_part, ff_part, 1)
+    gu_mine = jnp.concatenate(
+        [gate_mine[:, :whole], up_mine[:, :whole], gate_mine[:, whole:], up_mine[:, whole:]], axis=1
+    )
+    small = jnp.concatenate(
+        [
+            gain_attn.reshape(1, 128),
+            gain_mlp.reshape(1, 128),
+            b_qkv.reshape(3, 128),
+            jnp.zeros((11, 128), BF16),
+        ]
+    )
+    x_all, cot_all, small_all, wqkv, wout, wgu, wdown = gather_all(
+        inputs, cotangent, small, qkv_mine, w_out, gu_mine, w_down
+    )
+    small_all = small_all.reshape(count, 16, 128).astype(F32)
+    gain_one = small_all[:, 0].reshape(1, width)
+    gain_two = small_all[:, 1].reshape(1, width)
+    bias = lax.dynamic_index_in_dim(
+        small_all[:, 2:5].reshape(3, SEQ_PARTS, inner), quarter, 1, keepdims=False
+    ).reshape(1, 3 * inner)
+
+    cosine_tab, sine_tab = rope_tables(jnp.arange(tokens, dtype=jnp.int32))
+    cos_b, sin_b = cosine_tab[:, None, :], sine_tab[:, None, :]
+    hidden = x_all.astype(F32)
+    normed_low = rms_scale(hidden, gain_one).astype(BF16)
+    projected = jnp.dot(normed_low, wqkv, preferred_element_type=F32) + bias
+    pre = projected.reshape(tokens, 3, heads, HEAD_DIM)
+    queries = rotate(pre[:, 0], cos_b, sin_b).astype(BF16)
+    keys = rotate(pre[:, 1], cos_b, sin_b).astype(BF16)
+    values = pre[:, 2].astype(BF16)
+    attended, log_totals = attend_forward(queries, keys, values)
+    attended_flat = attended.reshape(tokens, inner)
+    mid, normed_two = middle_step(
+        jnp.dot(attended_flat, wout, preferred_element_type=F32), inputs, gain_two
+    )
+    both = jnp.dot(normed_two, wgu, preferred_element_type=F32)
+    gate = jnp.concatenate([both[:, :whole], both[:, 2 * whole : whole + ff_part]], axis=1)
+    up = jnp.concatenate([both[:, whole : 2 * whole], both[:, whole + ff_part :]], axis=1)
+    activated, act_pull = jax.vjp(lambda a, b: jax.nn.silu(a) * b, gate, up)
+    activated_low = activated.astype(BF16)
+    mlp_out = jnp.dot(activated_low, wdown, preferred_element_type=F32)
+    output = (mid + lax.psum_scatter(mlp_out, "seq", scatter_dimension=0, tiled=True)).astype(BF16)
+
+    grad_act = times_trans(cot_all, wdown)
+    grad_gate, grad_up = act_pull(grad_act)
+    grad_gu = jnp.concatenate(
+        [grad_gate[:, :whole], grad_up[:, :whole], grad_gate[:, whole:], grad_up[:, whole:]], axis=1
+    ).astype(BF16)
+    grad_mid, grad_mid_all, grad_gain_two = back_step(
+        times_trans(grad_gu, wgu), mid, cotangent, gain_two, 2
+    )
+    term_down = trans_times(activated_low, cot_all).astype(BF16)
+    term_gu = trans_times(normed_two, grad_gu).astype(BF16)
+    term_out = trans_times(attended_flat, grad_mid_all).astype(BF16)
+    grad_attended = times_trans(grad_mid_all, wout).astype(BF16).reshape(tokens, heads, HEAD_DIM)
+    grad_q, grad_k, grad_v = attend_backward(queries, keys, values, log_totals, grad_attended)
+    grad_proj = jnp.stack(
+        [
+            unrotate(grad_q.astype(F32), cos_b, sin_b),
+            unrotate(grad_k.astype(F32), cos_b, sin_b),
+            grad_v.astype(F32),
+        ],
+        axis=1,
+    ).reshape(tokens, 3 * inner).astype(BF16)
+    term_qkv = trans_times(normed_low, grad_proj).astype(BF16)
+    grad_inputs, _, grad_gain_one = back_step(
+        times_trans(grad_proj, wqkv), inputs.astype(F32), grad_mid, gain_one, 3
+    )
+    bias_rows = lax.dynamic_update_slice(
+        jnp.zeros((3, SEQ_PARTS, inner), F32),
+        jnp.sum(grad_proj.astype(F32), axis=0).reshape(3, 1, inner),
+        (0, quarter, 0),
+    ).reshape(count, 3, 128)
+    vector = jnp.concatenate(
+        [
+            grad_gain_one.reshape(count, 1, 128),
+            grad_gain_two.reshape(count, 1, 128),
+            bias_rows,
+            jnp.zeros((count, 3, 128), F32),
+        ],
+        axis=1,
+    ).reshape(count * 8, 128)
+    sums, sum_down, sum_gu, sum_out, sum_qkv = reduce_all(
+        vector, term_down, term_gu, term_out, term_qkv
+    )
+    order = [0, 2, 3, 1]
+    parts = [sum_gu[index].astype(F32) for index in order]
+    grad_w_gate = jnp.concatenate(
+        [piece for each in parts for piece in (each[:, :whole], each[:, 2 * whole : whole + ff_part])],
+        axis=1,
+    )
+    grad_w_up = jnp.concatenate(
+        [piece for each in parts for piece in (each[:, whole : 2 * whole], each[:, whole + ff_part :])],
+        axis=1,
+    )
+    grad_w_qkv = jnp.concatenate(
+        [sum_qkv[index, :, kind * inner : (kind + 1) * inner] for kind in range(3) for index in order],
+        axis=1,
+    ).astype(F32)
+    return (
+        output,
+        grad_inputs,
+        sums[0],
+        grad_w_qkv,
+        sums[2:5].reshape(-1),
+        sum_out.astype(F32),
+        sums[1],
+        grad_w_gate,
+        grad_w_up,
+        sum_down.astype(F32),
+    )
+
+
 def solution(mesh):
+    tuned = mesh.shape["dp"] == Z_LEN * X_LEN and mesh.shape["seq"] == SEQ_PARTS
     return jax.shard_map(
-        body,
+        ring_body if tuned else generic_body,
         mesh=mesh,
         in_specs=(
             P(("dp", "seq"), None),

time: 1040 us -> 429 us (0.41)
  waiting for transfers between devices: 770 us -> 0.02 us
  Pallas kernels: 0 us -> 319 us
  blocking collectives: 117 us -> 0 us
  matrix products: 67.6 us -> 39.3 us
  starting transfers between devices: 26 us -> 0.04 us
  local copies, waits for them, and re-layouts: 28.5 us -> 39 us
    reduce_scatter x4 -> x1, waiting for transfers between devices: 423 us -> 0.01 us  [ring_body(): lax.psum_scatter(mlp_out, 'seq', scatter_dimension=0, tiled=True)]
    pallas_call x0 -> x5, Pallas kernels: none -> 319 us  [the longest x1 136 us: reduce_all(): pl.pallas_call(reduce_kernel, out_shape=(jax.ShapeDtypeStruct((vector.sha...]
    all_gather x5 -> x0, waiting for transfers between devices: 308 us -> none  [the longest x1 87.9 us: body(): lax.all_gather(w_gate, 'dp', axis=0, tiled=True)]
    all_gather x3 -> x0, blocking collectives: 67.2 us -> none  [the longest x1 26.6 us: body(): lax.all_gather(b_qkv, 'dp', axis=0, tiled=True)]
    unnamed x1 -> x0, blocking collectives: 34.9 us -> none
    all_to_all x7 -> x0, starting transfers between devices: 25.3 us -> none  [the longest x1 4.26 us: body(): lax.all_to_all(grad_v, 'seq', split_axis=0, concat_axis=1, tiled=True)]
    all_to_all x7 -> x0, waiting for transfers between devices: 20.6 us -> none  [the longest x1 5.95 us: body(): lax.all_to_all(grad_attended.reshape(tokens, HEADS, HEAD_DIM), 'seq', spl...]
    psum x1 -> x0, waiting for transfers between devices: 15.1 us -> none  [body(): lax.psum(sum_wqkv.astype(jnp.bfloat16), 'seq').astype(jnp.float32)]
  transfers between devices with their start and end apart: 17 -> 1, of which waited for: 13 -> 0; matrix products, arithmetic and copies ran while one was open for 8% -> 13% of each run, Pallas kernels for 0% -> 48%
where the time goes in v1:
time: 429 us; the launch traced here: 426 us
  Pallas kernels  319 us (74%)
  matrix products  39.3 us (9%)
  local copies, waits for them, and re-layouts  39 us (9%)
  between operations  14.6 us (3%)
  other arithmetic  14.3 us (3%)
    pallas_call x1, Pallas kernels, reduce_all(): pl.pallas_call(reduce_kernel, out_shape=(jax.ShapeDtypeStruct((vector.sha...  136 us
    pallas_call x1, Pallas kernels, gather_all(): pl.pallas_call(gather_kernel, out_shape=(grown(x_in, SEQ_PARTS), grown(co...  84 us
    pallas_call x2, Pallas kernels, back_step(): pl.pallas_call(back_kernel, out_shape=(jax.ShapeDtypeStruct((rows, width)...  67.3 us
    pallas_call x1, Pallas kernels, middle_step(): pl.pallas_call(middle_kernel, out_shape=(jax.ShapeDtypeStruct((rows, widt...  31.8 us
    unnamed x83, local copies, waits for them, and re-layouts  17.2 us
    dot_general x4, matrix products, times_trans(): lax.dot_general(left_op, weight, (((1,), (1,)), ((), ())), preferred_elem...  12.2 us
    dot_general x4, matrix products, trans_times(): lax.dot_general(left_op, right_op, (((0,), (0,)), ((), ())), preferred_el...  9.07 us
  transfers between devices with their start and end apart: 1, of which 0 were waited for; matrix products, arithmetic and copies ran while one was open for 13% of the time, Pallas kernels for 48%

profile of v1, /device:TPU:0, one launch (start us, length us, event | category | flops | bytes accessed | tf_op | source)
XLA Modules:
  0.0 426.0 jit_solution(10503977113833498621)
XLA Ops:
  7.3 1.2 constant_dynamic-slice_fusion
  8.5 0.9 constant_dynamic-slice_fusion.2
  9.3 1.5 copy.44
  10.9 0.8 copy.45.qkv
  11.8 0.8 concatenate.49.gate_up
  12.6 0.7 maximum_maximum_fusion.small
  13.3 84.0 %shard_map.177 = (bf16[512,1024]{1,0:T(8,128)(2,1)}, bf16[512,1024]{1,0:T(8,128)(2,1)}, bf16[128,128]{1,0:T(8,128)(2,1)}, bf16[1024,768]{1,0:T(8,128)(2,1)}, bf1...) custom-call(bf16[128,1024]{1,0:T(8,128)(2,1)} %x_in.3, bf16[128,1024]{1,0:T(8,128)(2,1)} %base.1, ...), custom_call_target="tpu_custom_call" | custom-call | tf_op jit(solution)/shard_map/pallas_call | solution.py:550
  97.3 0.7 slice.250
  98.0 0.7 slice.249
  98.8 1.4 convert.27
  100.3 1.5 fusion.2
  102.4 2.8 convolution_add_fusion
  106.5 0.9 fusion.53
  108.0 1.4 copy-done
  109.4 0.8 fusion.28
  110.2 1.4 slice_bitcast_fusion.6
  111.7 1.9 fusion.54.partial
  113.6 31.8 %shard_map.178 = (f32[128,1024]{1,0:T(8,128)}, bf16[512,1024]{1,0:T(8,128)(2,1)}) custom-call(f32[512,1024]{1,0:T(8,128)} %fusion.54.partial, bf16[128,1024]{1,0:T(8,128)(2,1)} %x_in.3, f32[1,1024]{1,0:T(1,128)} %get-tuple-element.139.gain), custom_call_target="tpu_custom_call" | custom-call | tf_op jit(solution)/shard_map/pallas_call | solution.py:662
  145.3 3.9 fusion.55
  149.6 1.0 copy-done.29
  150.9 2.8 multiply_convert_fusion.1
  153.7 2.4 fusion.56
  156.2 1.2 slice.263
  157.3 1.6 slice.265
  158.9 1.1 slice.264
  160.0 1.6 slice.266
  161.6 3.1 concatenate.56
  164.8 5.4 %fusion.57.partial = f32[512,1024]{1,0:T(8,128)} fusion(bf16[512,1408]{1,0:T(8,128)(2,1)} %concatenate.56, bf16[1024,1408]{1,0:T(8,128)(2,1)} %get-tuple-element.80), kind=kOutput, calls=%fused_computation.122 | convolution fusion | flops 1476395008 | bytes 6422528 | tf_op jit(solution)/shard_map/dot_general | solution.py:51
  170.2 40.8 %shard_map.179 = (f32[128,1024]{1,0:T(8,128)}, bf16[512,1024]{1,0:T(8,128)(2,1)}, f32[1,1024]{1,0:T(1,128)}) custom-call(f32[512,1024]{1,0:T(8,128)} %fusion.57.partial, f32[128,1024]{1,0:T(8,128)} %get-tuple-element.78.mid, bf16[128,1024]{1,0:T(8,128)(2,1)} %base.1, f32[1,1024]{1,0:T(1,128)} %get-tuple-element.139.gain), custom_call_target="tpu_custom_call" | custom-call | tf_op jit(solution)/shard_map/pallas_call | solution.py:710
  211.0 1.7 convolution_convert_fusion.4
  212.7 3.3 multiply_reduce_fusion
  216.2 0.8 fusion.19
  217.4 1.2 convolution_convert_fusion.3.wout
  218.7 3.4 convolution_convert_fusion.gate_up
  222.1 1.2 multiply_convert_fusion
  223.3 0.8 fusion.27
  224.6 0.8 copy-done.7
  225.9 0.7 copy-done.9
  226.7 2.4 convolution_convert_fusion.1.qkv
  229.1 2.4 fusion.58.partial
  231.5 0.8 convert_element_type.194.mid
  232.3 2.0 convolution_convert_fusion.2.down
  234.6 26.5 %shard_map.180 = (f32[128,1024]{1,0:T(8,128)}, bf16[512,1024]{1,0:T(8,128)(2,1)}, f32[1,1024]{1,0:T(1,128)}) custom-call(f32[512,1024]{1,0:T(8,128)} %fusion.58.partial, f32[128,1024]{1,0:T(8,128)} %convert_element_type.194.mid, f32[128,1024]{1,0:T(8,128)} %get-tuple-element.84.base, f32[1,1024]{1,0:T(1,128)} %get-tuple-element.138.gain), custom_call_target="tpu_custom_call" | custom-call | tf_op jit(solution)/shard_map/pallas_call | solution.py:710
  261.1 1.4 maximum_bitcast_fusion.vector_in
  262.5 135.8 %shard_map.181 = (f32[8,128]{1,0:T(8,128)}, bf16[352,1024]{1,0:T(8,128)(2,1)}, bf16[4,128,1408]{2,1,0:T(8,128)(2,1)}, bf16[128,1024]{1,0:T(8,128)(2,1)}, bf16[4,128,768]{2,1,0:T(8,128)(2,1)}) custom-call(f32[64,128]{1,0:T(8,128)} %maximum_bitcast_fusion.vector_in, bf16[704,1024]{1,0:T(8,128)(2,1)} %convolution_convert_fusion.2.down, ...), custom_call_target="tpu_custom_call" | custom-call | tf_op jit(solution)/shard_map/pallas_call | solution.py:999
  398.2 0.9 bitcast_dynamic-update-slice_fusion.11
  399.2 0.8 bitcast_dynamic-update-slice_fusion.10
  400.0 0.8 bitcast_dynamic-update-slice_fusion.9
  400.9 0.8 bitcast_dynamic-update-slice_fusion.8
  401.7 0.8 bitcast_dynamic-update-slice_fusion.7
  402.5 0.8 bitcast_dynamic-update-slice_fusion.6
  403.4 0.8 bitcast_dynamic-update-slice_fusion.5
  404.2 0.8 bitcast_dynamic-update-slice_fusion.4
  405.1 0.8 bitcast_dynamic-update-slice_fusion.3
  405.9 0.8 bitcast_dynamic-update-slice_fusion.2
  406.8 0.8 bitcast_dynamic-update-slice_fusion.1
  407.6 0.8 bitcast_dynamic-update-slice_fusion
  408.5 1.3 convert_element_type.200
  409.8 1.3 convert_element_type.210
  411.0 0.8 convert_element_type.201
  412.7 1.4 concatenate.62
  414.1 1.4 concatenate.61
  416.6 1.8 add_convert_fusion
  418.4 0.8 copy.73
  (112 shorter events, 7.2 us)
Async XLA Ops:
  7.2 5.5 %copy-start.27 = (bf16[128]{0:T(256)(128)(2,1)S(1)}, bf16[128]{0:T(256)(128)(2,1)}, u32[]{:S(2)}) copy-start(bf16[128]{0:T(256)(128)(2,1)} %param.11) | copy-start | bytes 772
  7.2 5.4 %copy-start.26 = (bf16[128]{0:T(256)(128)(2,1)S(1)}, bf16[128]{0:T(256)(128)(2,1)}, u32[]{:S(2)}) copy-start(bf16[128]{0:T(256)(128)(2,1)} %param.15) | copy-start | bytes 772
  7.2 5.4 %copy-start.25 = (bf16[384]{0:T(512)(128)(2,1)S(1)}, bf16[384]{0:T(512)(128)(2,1)}, u32[]{:S(2)}) copy-start(bf16[384]{0:T(512)(128)(2,1)} %param.13) | copy-start | bytes 2308
  7.2 409.4 %reduce-scatter.2.cloned.1.call-start = ((), (), s32[]{:S(2)}) async-start(), calls=%async_computation.1 | async-start | bytes 2621440 | tf_op jit(solution)/shard_map/reduce_scatter | solution.py:1082
  98.7 3.1 copy-start.20
  101.8 0.6 copy-start.23
  106.2 1.2 copy-start.6
  107.4 2.0 copy-start
  109.4 0.8 copy-start.17
  109.4 2.3 copy-start.14
  110.2 35.1 %copy-start.10 = (bf16[4,64,512]{2,1,0:T(8,128)(2,1)}, bf16[4,64,512]{2,1,0:T(8,128)(2,1)S(1)}, u32[]{:S(2)}) copy-start(bf16[4,64,512]{2,1,0:T(8,128)(2,1)S(1)} %fusion.28) | copy-start | bytes 786436
  149.3 1.4 copy-start.29
  149.3 1.6 copy-start.30
  153.7 2.4 copy-start.33
  156.2 5.5 %copy-start.18 = (f32[4,512]{1,0:T(4,128)S(1)}, f32[4,512]{1,0:T(4,128)}, u32[]{:S(2)}) copy-start(f32[4,512]{1,0:T(4,128)} %copy-done.17) | copy-start | bytes 24580
  170.2 40.9 %copy-start.15 = (bf16[256,1024]{1,0:T(8,128)(2,1)S(1)}, bf16[256,1024]{1,0:T(8,128)(2,1)}, u32[]{:S(2)}) copy-start(bf16[256,1024]{1,0:T(8,128)(2,1)} %get-tuple-element.77) | copy-start | bytes 1572868
  212.7 3.5 copy-start.1
  216.2 1.2 copy-start.8
  216.2 1.3 copy-start.11
  216.2 2.5 copy-start.5
  216.2 2.5 copy-start.32
  224.5 0.9 copy-start.7
  225.4 1.2 copy-start.9
  225.4 1.2 copy-start.21
  225.4 1.2 copy-start.24
  226.7 2.4 copy-start.28
  229.1 2.4 copy-start.2
  229.1 3.2 copy-start.31
  229.1 3.2 copy-start.34
  234.4 26.7 %copy-start.19 = (f32[1,1024]{1,0:T(1,128)S(1)}, f32[1,1024]{1,0:T(1,128)}, u32[]{:S(2)}) copy-start(f32[1,1024]{1,0:T(1,128)} %get-tuple-element.87) | copy-start | bytes 12292
  398.2 11.5 %copy-start.12 = (bf16[352,1024]{1,0:T(8,128)(2,1)S(1)}, bf16[352,1024]{1,0:T(8,128)(2,1)}, u32[]{:S(2)}) copy-start(bf16[352,1024]{1,0:T(8,128)(2,1)} %get-tuple-element.92) | copy-start | bytes 2162692
  408.5 2.6 copy-start.16
  408.5 3.4 copy-start.4
  414.1 1.4 copy-start.22
  414.1 2.5 copy-start.3
  414.1 4.3 %copy-start.13 = (f32[128,1024]{1,0:T(8,128)S(1)}, f32[128,1024]{1,0:T(8,128)}, u32[]{:S(2)}) copy-start(f32[128,1024]{1,0:T(8,128)} %get-tuple-element.166) | copy-start | bytes 1572868
Sparse Core Ops, SparseCore 0:
  156.3 53.9 reduce-scatter.1

commit v2 on v0

--- a/solution.py
+++ b/solution.py
@@ -3,6 +3,8 @@
 import jax
 import jax.numpy as jnp
 from jax import lax
+from jax.experimental import pallas as pl
+from jax.experimental.pallas import tpu as pltpu
 from jax.sharding import PartitionSpec as P
 
 HEADS = 16
@@ -132,7 +134,7 @@
     )
 
 
-def body(inputs, gain_attn, w_qkv, b_qkv, w_out, gain_mlp, w_gate, w_up, w_down, cotangent):
+def generic_body(inputs, gain_attn, w_qkv, b_qkv, w_out, gain_mlp, w_gate, w_up, w_down, cotangent):
     tokens = inputs.shape[0]
     repeat = HEADS // KV_HEADS
     q_width = HEADS * HEAD_DIM
@@ -304,9 +306,1064 @@
     )
 
 
+Z_LEN = 4
+X_LEN = 2
+SEQ_PARTS = 4
+MESH = pl.DeviceIdType.MESH
+HBM = pl.BlockSpec(memory_space=pl.ANY)
+VMEM = pl.BlockSpec(memory_space=pltpu.VMEM)
+BF16 = jnp.bfloat16
+F32 = jnp.float32
+
+
+def place():
+    dp = lax.axis_index("dp")
+    part = lax.axis_index("seq")
+    z, x = lax.div(dp, X_LEN), lax.rem(dp, X_LEN)
+    return dp, part, z, x
+
+
+def quarter_of(part):
+    y, core = lax.div(part, 2), lax.rem(part, 2)
+    return (1 - y) * 3 * core + y * (1 + core)
+
+
+def turn(value, step, length):
+    return lax.rem(value + step, length)
+
+
+def remote(source, target, send, recv, dp, part):
+    return pltpu.make_async_remote_copy(
+        src_ref=source,
+        dst_ref=target,
+        send_sem=send,
+        recv_sem=recv,
+        device_id=(dp, part),
+        device_id_type=MESH,
+    )
+
+
+def block(index, size):
+    return pl.ds(pl.multiple_of(index * size, size), size)
+
+
+def greet(partners):
+    barrier = pltpu.get_barrier_semaphore()
+    for dp, part in partners:
+        pl.semaphore_signal(barrier, inc=1, device_id=(dp, part), device_id_type=MESH)
+    pl.semaphore_wait(barrier, len(partners))
+
+
+def z_partners(dp, part, z, x):
+    return [(turn(z, step, Z_LEN) * X_LEN + x, part) for step in range(1, Z_LEN)]
+
+
+def seq_partners(dp, part):
+    return [(dp, turn(part, step, SEQ_PARTS)) for step in range(1, SEQ_PARTS)]
+
+
+class RowGather:
+    def __init__(self, source, dest, send, recv, local, base):
+        self.source, self.dest, self.send, self.recv, self.local, self.base = (
+            source, dest, send, recv, local, base,
+        )
+        self.rows = dest.shape[0] // X_LEN
+
+    def slot(self, x):
+        return self.dest.at[block(x, self.rows)]
+
+    def copy(self, source, slot, send, recv, dp, part):
+        return remote(
+            source, slot, self.send.at[self.base + send], self.recv.at[self.base + recv], dp, part
+        )
+
+    def start(self):
+        dp, part, z, x = place()
+        quarter = quarter_of(part)
+        mine = self.slot(x)
+
+        @pl.when(z == quarter)
+        def _():
+            pltpu.make_async_copy(self.source, mine, self.local).start()
+            for step in range(1, Z_LEN):
+                self.copy(
+                    self.source, mine, step - 1, 0, turn(z, step, Z_LEN) * X_LEN + x, part
+                ).start()
+            self.copy(self.source, mine, 3, 1, z * X_LEN + 1 - x, part).start()
+
+    def relay(self):
+        dp, part, z, x = place()
+        mine = self.slot(x)
+
+        @pl.when(z != quarter_of(part))
+        def _():
+            self.copy(mine, mine, 0, 0, dp, part).wait_recv()
+            self.copy(mine, mine, 3, 1, z * X_LEN + 1 - x, part).start()
+
+    def arrive(self):
+        dp, part, z, x = place()
+        mine, other = self.slot(x), self.slot(1 - x)
+
+        @pl.when(z == quarter_of(part))
+        def _():
+            pltpu.make_async_copy(self.source, mine, self.local).wait()
+
+        self.copy(other, other, 3, 1, dp, part).wait_recv()
+
+    def drain(self):
+        dp, part, z, x = place()
+        mine = self.slot(x)
+
+        @pl.when(z == quarter_of(part))
+        def _():
+            for step in range(1, Z_LEN):
+                self.copy(self.source, mine, step - 1, 0, dp, part).wait_send()
+
+        self.copy(self.source, mine, 3, 1, dp, part).wait_send()
+
+
+def over_rows(count, step, work):
+    def one(index, carry):
+        work(pl.ds(pl.multiple_of(index * step, step), step))
+        return carry
+
+    lax.fori_loop(0, count // step, one, 0)
+
+
+def mean_square(value):
+    return lax.rsqrt(jnp.mean(value * value, axis=-1, keepdims=True) + NORM_EPS)
+
+
+def rms_back(value, grad, gain):
+    scale = mean_square(value)
+    unit = value * scale
+    pulled = grad * gain
+    inner = jnp.mean(pulled * unit, axis=-1, keepdims=True)
+    return scale * (pulled - unit * inner), grad * unit
+
+
+NT = (((1,), (1,)), ((), ()))
+NN = (((1,), (0,)), ((), ()))
+
+
+def dot(left, right, dims=NN):
+    return lax.dot_general(left, right, dims, preferred_element_type=F32)
+
+
+def loop(count, work):
+    def one(index, carry):
+        work(index)
+        return carry
+
+    lax.fori_loop(0, count, one, 0)
+
+
+def lanes(rows):
+    return lax.broadcasted_iota(jnp.int32, (rows, 128), 1)
+
+
+def turned(value):
+    low_half = lax.rem(lanes(value.shape[0]), HEAD_DIM) < HEAD_DIM // 2
+    return jnp.where(low_half, -pltpu.roll(value, 96, axis=1), pltpu.roll(value, 32, axis=1))
+
+
+def turned_back(value):
+    low_half = lax.rem(lanes(value.shape[0]), HEAD_DIM) < HEAD_DIM // 2
+    return jnp.where(low_half, pltpu.roll(value, 96, axis=1), -pltpu.roll(value, 32, axis=1))
+
+
+def sigmoid(value):
+    return 1.0 / (1.0 + jnp.exp(-value))
+
+
+def transpose_into(target, source):
+    def work(index):
+        target[block(index, 128), :] = source[:, block(index, 128)].T
+
+    loop(source.shape[1] // 128, work)
+
+
+class ColumnGather:
+    def __init__(self, dest, send, recv, base):
+        self.dest, self.send, self.recv, self.base = dest, send, recv, base
+        self.rows = dest.shape[0] // (Z_LEN * X_LEN)
+
+    def slot(self, dp):
+        return self.dest.at[block(dp, self.rows)]
+
+    def copy(self, slot, index, dp, part):
+        return remote(
+            slot, slot, self.send.at[self.base + index], self.recv.at[self.base + index], dp, part
+        )
+
+    def start_z(self):
+        dp, part, z, x = place()
+        for step in range(1, Z_LEN):
+            self.copy(self.slot(dp), step - 1, turn(z, step, Z_LEN) * X_LEN + x, part).start()
+
+    def start_x(self):
+        dp, part, z, x = place()
+        self.copy(self.slot(dp), 3, z * X_LEN + 1 - x, part).start()
+
+    def relay(self, steps=range(1, Z_LEN)):
+        dp, part, z, x = place()
+        for step in steps:
+            slot = self.slot(turn(z, Z_LEN - step, Z_LEN) * X_LEN + x)
+            self.copy(slot, step - 1, dp, part).wait_recv()
+            self.copy(slot, 3 + step, z * X_LEN + 1 - x, part).start()
+
+    def arrive(self):
+        dp, part, z, x = place()
+        for step in range(Z_LEN):
+            slot = self.slot(turn(z, Z_LEN - step, Z_LEN) * X_LEN + 1 - x)
+            self.copy(slot, 3 + step, dp, part).wait_recv()
+
+    def drain(self):
+        dp, part, z, x = place()
+        for index in range(7):
+            self.copy(self.slot(dp), index, dp, part).wait_send()
+
+
+class SeqGather:
+    def __init__(self, dest, send, recv, base):
+        self.dest, self.send, self.recv, self.base = dest, send, recv, base
+        self.rows = dest.shape[0] // SEQ_PARTS
+
+    def copy(self, slot, index, dp, part):
+        where = self.dest.at[block(slot, self.rows)]
+        return remote(
+            where, where, self.send.at[self.base + index], self.recv.at[self.base + index], dp, part
+        )
+
+    def start(self):
+        dp, part, z, x = place()
+        for step in range(1, SEQ_PARTS):
+            self.copy(part, step - 1, dp, turn(part, step, SEQ_PARTS)).start()
+
+    def arrive(self):
+        dp, part, z, x = place()
+        for step in range(1, SEQ_PARTS):
+            self.copy(turn(part, SEQ_PARTS - step, SEQ_PARTS), step - 1, dp, part).wait_recv()
+
+    def drain(self):
+        dp, part, z, x = place()
+        for step in range(1, SEQ_PARTS):
+            self.copy(part, step - 1, dp, part).wait_send()
+
+
+class SeqReduce:
+    def __init__(self, own, outbox, inbox, send, recv, base):
+        self.own, self.outbox, self.inbox = own, outbox, inbox
+        self.send, self.recv, self.base = send, recv, base
+
+    def copy(self, index, dp, part):
+        return remote(
+            self.outbox.at[index],
+            self.inbox.at[index],
+            self.send.at[self.base + index],
+            self.recv.at[self.base + index],
+            dp,
+            part,
+        )
+
+    def start(self, left, right, dims):
+        dp, part, z, x = place()
+        rows = self.own.shape[0]
+        for first in (1, 3):
+            near, far = [turn(part, first + each, SEQ_PARTS) for each in range(2)]
+            both = jnp.concatenate([left[block(near, rows), :], left[block(far, rows), :]], axis=0)
+            value = dot(both, right[...], dims)
+            self.outbox[first - 1] = value[:rows].astype(BF16)
+            self.copy(first - 1, dp, near).start()
+            if first == 1:
+                self.outbox[first] = value[rows:].astype(BF16)
+                self.copy(first, dp, far).start()
+            else:
+                self.own[...] = value[rows:]
+
+    def arrive(self):
+        dp, part, z, x = place()
+        for step in range(SEQ_PARTS - 1):
+            self.copy(step, dp, part).wait_recv()
+
+    def total(self, rows):
+        value = self.own[rows, :]
+        for step in range(SEQ_PARTS - 1):
+            value = value + self.inbox[step, rows, :].astype(F32)
+        return value
+
+    def drain(self):
+        dp, part, z, x = place()
+        for step in range(SEQ_PARTS - 1):
+            self.copy(step, dp, part).wait_send()
+
+
+class ColumnReduce:
+    def __init__(self, outbox, keep, xbox, hold, zbox, send, recv, base):
+        self.outbox, self.keep, self.xbox, self.hold, self.zbox = outbox, keep, xbox, hold, zbox
+        self.send, self.recv, self.base = send, recv, base
+        self.rows = keep.shape[1]
+
+    def copy(self, source, slot, index, dp, part):
+        return remote(
+            source, slot, self.send.at[self.base + index], self.recv.at[self.base + index], dp, part
+        )
+
+    def cross(self, step):
+        dp, part, z, x = place()
+        return self.copy(
+            self.outbox.at[step], self.xbox.at[step], step, z * X_LEN + 1 - x, part
+        )
+
+    def along(self, step):
+        dp, part, z, x = place()
+        return self.copy(
+            self.hold.at[step - 1],
+            self.zbox.at[step - 1],
+            3 + step,
+            turn(z, step, Z_LEN) * X_LEN + x,
+            part,
+        )
+
+    def start(self, left, right):
+        dp, part, z, x = place()
+        for step in range(Z_LEN - 1, -1, -1):
+            target = turn(z, step, Z_LEN) * X_LEN
+            both = jnp.concatenate(
+                [left[block(target + 1 - x, self.rows), :], left[block(target + x, self.rows), :]],
+                axis=0,
+            )
+            value = dot(both, right[...])
+            self.outbox[step] = value[: self.rows].astype(BF16)
+            self.cross(step).start()
+            self.keep[step] = value[self.rows :]
+
+    def relay(self, step):
+        self.cross(step).wait_recv()
+
+        def work(rows):
+            value = self.keep[step, rows, :] + self.xbox[step, rows, :].astype(F32)
+            if step:
+                self.hold[step - 1, rows, :] = value.astype(BF16)
+            else:
+                self.keep[step, rows, :] = value
+
+        over_rows(self.rows, 16, work)
+        if step:
+            self.along(step).start()
+
+    def arrive(self):
+        for step in range(1, Z_LEN):
+            self.along(step).wait_recv()
+
+    def total(self, rows):
+        value = self.keep[0, rows, :]
+        for step in range(Z_LEN - 1):
+            value = value + self.zbox[step, rows, :].astype(F32)
+        return value.astype(BF16)
+
+    def drain(self):
+        for step in range(Z_LEN):
+            self.cross(step).wait_send()
+        for step in range(1, Z_LEN):
+            self.along(step).wait_send()
+
+
+class RowReduce:
+    def __init__(self, grads, outbox, xbox, hold, zbox, out, send, recv, base):
+        self.grads, self.outbox, self.xbox = grads, outbox, xbox
+        self.hold, self.zbox, self.out = hold, zbox, out
+        self.send, self.recv, self.base = send, recv, base
+        self.rows = out.shape[0]
+
+    def copy(self, source, slot, send, recv, dp, part):
+        return remote(
+            source, slot, self.send.at[self.base + send], self.recv.at[self.base + recv], dp, part
+        )
+
+    def cross(self):
+        dp, part, z, x = place()
+        return self.copy(self.outbox, self.xbox, 0, 0, z * X_LEN + 1 - x, part)
+
+    def along(self, step):
+        dp, part, z, x = place()
+        return self.copy(
+            self.hold, self.zbox.at[step - 1], 1, 1 + step, quarter_of(part) * X_LEN + x, part
+        )
+
+    def share(self, step, source_part):
+        dp, part, z, x = place()
+        return self.copy(self.out, self.out, 1 + step, 5, dp, turn(source_part, step, SEQ_PARTS))
+
+    def here(self, x, rows):
+        return pl.ds(pl.multiple_of(x * self.rows + rows.start, 16), 16)
+
+    def start(self):
+        dp, part, z, x = place()
+
+        def work(rows):
+            self.outbox[rows, :] = self.grads[self.here(1 - x, rows), :].astype(BF16)
+
+        over_rows(self.rows, 16, work)
+        self.cross().start()
+
+    def relay(self):
+        dp, part, z, x = place()
+        self.cross().wait_recv()
+        gap = turn(quarter_of(part), Z_LEN - z, Z_LEN)
+
+        def value(rows):
+            return self.grads[self.here(x, rows), :] + self.xbox[rows, :].astype(F32)
+
+        @pl.when(gap == 0)
+        def _():
+            def work(rows):
+                self.grads[self.here(x, rows), :] = value(rows)
+
+            over_rows(self.rows, 16, work)
+
+        @pl.when(gap != 0)
+        def _():
+            def work(rows):
+                self.hold[rows, :] = value(rows).astype(BF16)
+
+            over_rows(self.rows, 16, work)
+
+        for step in range(1, Z_LEN):
+
+            @pl.when(gap == step)
+            def _(step=step):
+                self.along(step).start()
+
+    def finish(self):
+        dp, part, z, x = place()
+
+        @pl.when(z == quarter_of(part))
+        def _():
+            for step in range(1, Z_LEN):
+                self.along(step).wait_recv()
+
+            def work(rows):
+                value = self.grads[self.here(x, rows), :]
+                for step in range(Z_LEN - 1):
+                    value = value + self.zbox[step, rows, :].astype(F32)
+                self.out[rows, :] = value.astype(BF16)
+
+            over_rows(self.rows, 16, work)
+            for step in range(1, SEQ_PARTS):
+                self.share(step, part).start()
+
+    def drain(self):
+        dp, part, z, x = place()
+        self.cross().wait_send()
+
+        @pl.when(z == quarter_of(part))
+        def _():
+            for step in range(1, SEQ_PARTS):
+                self.share(step, part).wait_send()
+
+        @pl.when(z != quarter_of(part))
+        def _():
+            self.along(1).wait_send()
+            self.copy(self.out, self.out, 1, 5, dp, part).wait_recv()
+
+
+class VectorReduce:
+    def __init__(self, vector, seq_box, dp_box, out, send, recv, base):
+        self.vector, self.seq_box, self.dp_box, self.out = vector, seq_box, dp_box, out
+        self.send, self.recv, self.base = send, recv, base
+        self.rows = vector.shape[0] // (Z_LEN * X_LEN)
+
+    def copy(self, source, slot, index, dp, part):
+        return remote(
+            source, slot, self.send.at[self.base + index], self.recv.at[self.base + index], dp, part
+        )
+
+    def near(self, step):
+        dp, part, z, x = place()
+        return self.copy(
+            self.seq_box.at[part], self.seq_box.at[part], step, dp, turn(part, step, SEQ_PARTS)
+        )
+
+    def far(self, step):
+        dp, part, z, x = place()
+        target = turn(dp, step, Z_LEN * X_LEN)
+        return self.copy(
+            self.vector.at[block(target, self.rows)], self.dp_box.at[dp], 4 + step, target, part
+        )
+
+    def start(self):
+        dp, part, z, x = place()
+        self.seq_box[part] = self.vector[...]
+        for step in range(1, SEQ_PARTS):
+            self.near(step).start()
+
+    def relay(self):
+        dp, part, z, x = place()
+        for step in range(1, SEQ_PARTS):
+            slot = self.seq_box.at[turn(part, SEQ_PARTS - step, SEQ_PARTS)]
+            self.copy(slot, slot, step, dp, part).wait_recv()
+        value = self.seq_box[0]
+        for step in range(1, SEQ_PARTS):
+            value = value + self.seq_box[step]
+        self.vector[...] = value
+        self.dp_box[dp] = self.vector[block(dp, self.rows), :]
+        for step in range(1, Z_LEN * X_LEN):
+            self.far(step).start()
+
+    def finish(self):
+        dp, part, z, x = place()
+        count = Z_LEN * X_LEN
+        for step in range(1, count):
+            slot = self.dp_box.at[turn(dp, count - step, count)]
+            self.copy(slot, slot, 4 + step, dp, part).wait_recv()
+        value = self.dp_box[0]
+        for step in range(1, count):
+            value = value + self.dp_box[step]
+        self.out[...] = value
+
+    def drain(self):
+        for step in range(1, SEQ_PARTS):
+            self.near(step).wait_send()
+        for step in range(1, Z_LEN * X_LEN):
+            self.far(step).wait_send()
+
+
+class Share:
+    def __init__(self, piece_of, send, recv, base):
+        self.piece_of, self.send, self.recv, self.base = piece_of, send, recv, base
+
+    def copy(self, index, owner, dp, part):
+        piece = self.piece_of(owner)
+        return remote(
+            piece, piece, self.send.at[self.base + index], self.recv.at[self.base + index], dp, part
+        )
+
+    def start(self):
+        dp, part, z, x = place()
+        for step in range(1, SEQ_PARTS):
+            self.copy(step - 1, part, dp, turn(part, step, SEQ_PARTS)).start()
+
+    def finish(self):
+        dp, part, z, x = place()
+        for step in range(1, SEQ_PARTS):
+            self.copy(step - 1, turn(part, SEQ_PARTS - step, SEQ_PARTS), dp, part).wait_recv()
+        for step in range(1, SEQ_PARTS):
+            self.copy(step - 1, part, dp, part).wait_send()
+
+
+def layer_kernel(
+    x_in, cot, small, w_qkv, w_out, w_gate, w_up, w_down, cos_ref, sin_ref,
+    out, grad_in, vec_out, o_qkv, o_out, o_gate, o_up, o_down,
+    x_all, cot_all, small_all, small_f, gains, bias_rows, edge, wqkv, wout, wgu, wdown,
+    n1, n1t, n2, n2t, gb, q_b, k_b, v_b, qt, att, att_t, norm_log, mid,
+    gu_f, act, act_t, ggu, down_f, wout_f, g_att, gat, gpr, gkt, gvt, gmid,
+    own_mid, own_gn2, own_out, own_gn1, outbox, inbox,
+    down_o, down_x, down_h, down_z, gu_o, gu_k, gu_x, gu_h, gu_z,
+    wout_o, wout_x, wout_h, wout_z, qkv_o, qkv_k, qkv_x, qkv_h, qkv_z,
+    tail_box, gain_sum, vector, seq_box, dp_box, send, recv, local,
+):
+    dp, part, z, x = place()
+    quarter = quarter_of(part)
+    odd = lax.rem(quarter, 2)
+    rows = x_in.shape[0]
+    width = x_in.shape[1]
+    tokens = rows * SEQ_PARTS
+    inner = wout.shape[0]
+    ff_part = w_gate.shape[1] // SEQ_PARTS
+    whole = ff_part // 128 * 128
+    padded = act.shape[1]
+    half = 64
+    own_rows = block(part, rows)
+
+    greet(
+        [(turn(dp, step, Z_LEN * X_LEN), part) for step in range(1, Z_LEN * X_LEN)]
+        + seq_partners(dp, part)
+    )
+
+    loads = []
+
+    def load(source, target):
+        copy = pltpu.make_async_copy(source, target, local.at[len(loads)])
+        copy.start()
+        loads.append(copy)
+        return copy
+
+    def gate_start(q):
+        return pl.multiple_of(q * ff_part + half * lax.rem(q, 2), 128)
+
+    def edge_start(q):
+        return pl.multiple_of(lax.div(q, 2) * 2 * ff_part + whole, 128)
+
+    load(x_in, x_all.at[own_rows])
+    load(small, small_all.at[block(dp, small.shape[0])])
+    for kind in range(3):
+        load(
+            w_qkv.at[:, pl.ds(pl.multiple_of(kind * width + quarter * inner, 128), inner)],
+            wqkv.at[block(dp, w_qkv.shape[0]), pl.ds(kind * inner, inner)],
+        )
+    load(cot, cot_all.at[own_rows])
+    for kind, source in enumerate((w_gate, w_up)):
+        load(
+            source.at[:, pl.ds(gate_start(quarter), whole)],
+            wgu.at[block(dp, source.shape[0]), pl.ds(kind * whole, whole)],
+        )
+    for kind, source in enumerate((w_gate, w_up)):
+        load(source.at[:, pl.ds(edge_start(quarter), 128)], edge.at[kind])
+
+    x_move = SeqGather(x_all, send, recv, 0)
+    cot_move = SeqGather(cot_all, send, recv, 3)
+    small_move = ColumnGather(small_all, send, recv, 8)
+    qkv_move = ColumnGather(wqkv, send, recv, 16)
+    wout_move = RowGather(w_out, wout, send, recv, local.at[14], 24)
+    gu_move = ColumnGather(wgu, send, recv, 32)
+    wdown_move = RowGather(w_down, wdown.at[pl.ds(0, ff_part)], send, recv, local.at[15], 40)
+
+    loads[0].wait()
+    x_move.start()
+    loads[1].wait()
+    small_move.start_z()
+    small_move.start_x()
+    for each in loads[2:5]:
+        each.wait()
+    qkv_move.start_z()
+    qkv_move.start_x()
+    wout_move.start()
+    for each in loads[5:]:
+        each.wait()
+    cot_move.start()
+    low_lanes = lanes(w_gate.shape[0]) < half
+    gate_edge, up_edge = edge[0].astype(F32), edge[1].astype(F32)
+    even_edge = jnp.where(low_lanes, gate_edge, pltpu.roll(up_edge, half, axis=1))
+    odd_edge = jnp.where(low_lanes, pltpu.roll(gate_edge, half, axis=1), up_edge)
+    wgu[block(dp, w_gate.shape[0]), pl.ds(2 * whole, 128)] = jnp.where(
+        odd == 0, even_edge, odd_edge
+    ).astype(BF16)
+    small_move.relay()
+    gu_move.start_z()
+    wdown_move.start()
+    small_move.arrive()
+
+    small_f[...] = small_all[...].astype(F32)
+    step16 = small.shape[0]
+    for shard in range(Z_LEN * X_LEN):
+        for kind in range(2):
+            gains[pl.ds(kind, 1), pl.ds(shard * 128, 128)] = small_f[
+                pl.ds(shard * step16 + kind, 1), :
+            ]
+        for kind in range(3):
+            bias_rows[pl.ds(shard * 3 + kind, 1), :] = small_f[
+                pl.ds(shard * step16 + 2 + kind, 1), :
+            ]
+    gain_one, gain_two = gains[pl.ds(0, 1), :], gains[pl.ds(1, 1), :]
+
+    x_move.arrive()
+
+    def norm_one(rows_now):
+        value = x_all[rows_now, :].astype(F32)
+        n1[rows_now, :] = (value * mean_square(value) * gain_one).astype(BF16)
+
+    over_rows(tokens, 32, norm_one)
+    transpose_into(n1t, n1)
+    qkv_move.relay()
+    gu_move.start_x()
+    qkv_move.arrive()
+
+    def project(rows_now):
+        for kind, target in enumerate((q_b, k_b, v_b)):
+            value = dot(n1[rows_now, :], wqkv[:, pl.ds(kind * inner, inner)])
+            for piece in range(inner // 128):
+                row = kind * (width // 128) + quarter * (inner // 128) + piece
+                bit = value[:, piece * 128 : piece * 128 + 128] + bias_rows[pl.ds(row, 1), :]
+                if kind < 2:
+                    bit = bit * cos_ref[rows_now, :] + turned(bit) * sin_ref[rows_now, :]
+                target[rows_now, pl.ds(piece * 128, 128)] = bit.astype(BF16)
+
+    over_rows(tokens, 256, project)
+    wout_move.relay()
+
+    scale = 1.0 / math.sqrt(HEAD_DIM)
+    span = tokens // 2
+
+    def head_parts(head):
+        tile = block(lax.div(head, 2), 128)
+        mask = lax.div(lanes(span), HEAD_DIM) == lax.rem(head, 2)
+        return tile, mask
+
+    def scores(query_rows, keys, first):
+        value = dot(query_rows, keys, NT) * scale
+        row = lax.broadcasted_iota(jnp.int32, value.shape, 0) + first
+        column = lax.broadcasted_iota(jnp.int32, value.shape, 1)
+        return jnp.where(row >= column, value, MASK_LOW)
+
+    def forward_head(head):
+        tile, mask = head_parts(head)
+        for first in (0, span):
+            near = pl.ds(first, span)
+            seen = pl.ds(0, first + span)
+            query_rows = jnp.where(mask, q_b[near, tile], jnp.zeros((), BF16))
+            value = scores(query_rows, k_b[seen, tile], first)
+            top = jnp.max(value, axis=-1, keepdims=True)
+            lifted = jnp.exp(value - top)
+            total = jnp.sum(lifted, axis=-1, keepdims=True)
+            chances = (lifted / total).astype(BF16)
+            result = dot(chances, v_b[seen, tile]).astype(BF16)
+            att[near, tile] = jnp.where(mask, result, att[near, tile])
+            norm_log[head, near, :] = jnp.broadcast_to(top + jnp.log(total), (span, 128))
+
+    att[...] = jnp.zeros_like(att)
+    loop(HEADS // SEQ_PARTS, forward_head)
+    wout_move.arrive()
+
+    mid_move = SeqReduce(own_mid, outbox.at[0], inbox.at[0], send, recv, 48)
+    mid_move.start(att, wout, NN)
+    transpose_into(att_t, att)
+    transpose_into(qt, q_b)
+    cot_move.arrive()
+    mid_move.arrive()
+    n2_move = SeqGather(n2, send, recv, 51)
+
+    def norm_two(rows_now):
+        here = pl.ds(pl.multiple_of(part * rows + rows_now.start, 16), 16)
+        value = x_all[here, :].astype(F32) + mid_move.total(rows_now)
+        mid[rows_now, :] = value
+        n2[here, :] = (value * mean_square(value) * gain_two).astype(BF16)
+
+    over_rows(rows, 16, norm_two)
+    n2_move.start()
+    n2_move.arrive()
+    transpose_into(n2t, n2)
+    gu_move.relay()
+    gu_move.arrive()
+
+    def feed(rows_now):
+        value = dot(n2[rows_now, :], wgu[...])
+        gu_f[rows_now, :] = value
+        gate, up = value[:, :whole], value[:, whole : 2 * whole]
+        act[rows_now, pl.ds(0, whole)] = (gate * sigmoid(gate) * up).astype(BF16)
+        last = value[:, 2 * whole :]
+        low = lanes(last.shape[0]) < half
+        product = last * sigmoid(last) * pltpu.roll(last, half, axis=1)
+        act[rows_now, pl.ds(whole, 128)] = jnp.where(low, product, 0.0).astype(BF16)
+
+    over_rows(tokens, 256, feed)
+    transpose_into(act_t, act)
+    down_move = RowReduce(down_f, down_o, down_x, down_h, down_z, o_down, send, recv, 60)
+
+    front = pl.multiple_of(half * odd, half)
+
+    def down_term(index):
+        value = dot(act_t[block(index, 256), :], cot_all[...])
+        down_f[pl.ds(pl.multiple_of(front + index * 256, half), 256), :] = value
+
+    loop(whole // 256, down_term)
+    value = dot(act_t[pl.ds(whole // 256 * 256, 256), :], cot_all[...])
+    down_f[pl.ds(pl.multiple_of(front + whole // 256 * 256, half), 128), :] = value[:128]
+    down_f[pl.ds(pl.multiple_of((1 - odd) * whole, half), half), :] = value[128 : 128 + half]
+    down_move.start()
+
+    wdown_move.relay()
+    wdown_move.arrive()
+    wdown[pl.ds(ff_part, half), :] = wdown[pl.ds(0, half), :]
+    wdown[pl.ds(ff_part + half, half), :] = jnp.zeros((half, width), BF16)
+    down_view = wdown.at[pl.ds(front, padded)]
+
+    def feed_back(rows_now):
+        grad = dot(cot_all[rows_now, :], down_view[...], NT)
+        value = gu_f[rows_now, :]
+        gate, up = value[:, :whole], value[:, whole : 2 * whole]
+        some = sigmoid(gate)
+        grad_whole = grad[:, :whole]
+        ggu[rows_now, pl.ds(0, whole)] = (
+            grad_whole * up * (some * (1.0 + gate * (1.0 - some)))
+        ).astype(BF16)
+        ggu[rows_now, pl.ds(whole, whole)] = (grad_whole * (gate * some)).astype(BF16)
+        last = value[:, 2 * whole :]
+        swapped = pltpu.roll(last, half, axis=1)
+        grad_last = grad[:, whole:]
+        low = lanes(last.shape[0]) < half
+        some = sigmoid(last)
+        ggu[rows_now, pl.ds(2 * whole, 128)] = jnp.where(
+            low,
+            grad_last * swapped * (some * (1.0 + last * (1.0 - some))),
+            pltpu.roll(grad_last, half, axis=1) * (swapped * sigmoid(swapped)),
+        ).astype(BF16)
+
+    over_rows(tokens, 128, feed_back)
+    gn2_move = SeqReduce(own_gn2, outbox.at[1], inbox.at[1], send, recv, 66)
+    gn2_move.start(ggu, wgu, NT)
+    gu_grad = ColumnReduce(gu_o, gu_k, gu_x, gu_h, gu_z, send, recv, 72)
+    gu_grad.start(n2t, ggu)
+    down_move.relay()
+    out_move = SeqReduce(own_out, outbox.at[2], inbox.at[2], send, recv, 80)
+    out_move.start(act, down_view, NN)
+
+    gn2_move.arrive()
+    gb_move = SeqGather(gb, send, recv, 84)
+    gain_sum[...] = jnp.zeros_like(gain_sum)
+
+    def mid_back(rows_now):
+        here = pl.ds(pl.multiple_of(part * rows + rows_now.start, 16), 16)
+        pulled, summand = rms_back(mid[rows_now, :], gn2_move.total(rows_now), gain_two)
+        total = cot_all[here, :].astype(F32) + pulled
+        gmid[rows_now, :] = total
+        gb[here, :] = total.astype(BF16)
+        gain_sum[pl.ds(8, 8), :] += jnp.sum(summand.reshape(2, 8, width), axis=0)
+
+    over_rows(rows, 16, mid_back)
+    gb_move.start()
+    gu_grad.relay(3)
+    out_move.arrive()
+
+    def emit(rows_now):
+        out[rows_now, :] = (mid[rows_now, :] + out_move.total(rows_now)).astype(BF16)
+
+    over_rows(rows, 16, emit)
+    gb_move.arrive()
+
+    def att_back(rows_now):
+        g_att[rows_now, :] = dot(gb[rows_now, :], wout[...], NT).astype(BF16)
+
+    over_rows(tokens, 256, att_back)
+    transpose_into(gat, g_att)
+    gu_grad.relay(2)
+
+    def backward_head(head):
+        tile, mask = head_parts(head)
+        mine = block(head, HEAD_DIM)
+        for first in (0, span):
+            near = pl.ds(first, span)
+            seen = pl.ds(0, first + span)
+            query_rows = jnp.where(mask, q_b[near, tile], jnp.zeros((), BF16))
+            value = scores(query_rows, k_b[seen, tile], first)
+            log_total = norm_log[head, near, :][:, :1]
+            chances = jnp.exp(value - log_total)
+            part_v = dot(gat[mine, near], chances.astype(BF16))
+            grad_rows = jnp.where(mask, g_att[near, tile], jnp.zeros((), BF16))
+            grad_chances = dot(grad_rows, v_b[seen, tile], NT)
+            inner_sum = jnp.sum(chances * grad_chances, axis=-1, keepdims=True)
+            grad_scores = (chances * (grad_chances - inner_sum)).astype(BF16)
+            part_q = dot(grad_scores, k_b[seen, tile]) * scale
+            part_q = part_q.astype(BF16).astype(F32)
+            old = gpr[near, tile].astype(F32)
+            gpr[near, tile] = jnp.where(mask, part_q, old).astype(BF16)
+            part_k = dot(qt[mine, near], grad_scores) * scale
+            if first == 0:
+                gkt[mine, pl.ds(0, span)] = part_k
+                gvt[mine, pl.ds(0, span)] = part_v
+            else:
+                gkt[mine, pl.ds(0, span)] += part_k[:, :span]
+                gvt[mine, pl.ds(0, span)] += part_v[:, :span]
+                gkt[mine, pl.ds(span, span)] = part_k[:, span:]
+                gvt[mine, pl.ds(span, span)] = part_v[:, span:]
+
+    gpr[:, pl.ds(0, inner)] = jnp.zeros((tokens, inner), BF16)
+    per_half = HEADS // SEQ_PARTS // 2
+    loop(per_half, backward_head)
+    gu_grad.relay(1)
+    loop(per_half, lambda head: backward_head(head + per_half))
+
+    def settle(index):
+        tile = block(index, 128)
+        for kind, source in ((1, gkt), (2, gvt)):
+            value = source[tile, :].astype(BF16).T
+            gpr[:, pl.ds(pl.multiple_of(kind * inner + index * 128, 128), 128)] = value
+
+    loop(inner // 128, settle)
+
+    def unturn(index):
+        tile = block(index, 128)
+        value = gpr[:, tile].astype(F32)
+        gpr[:, tile] = (
+            value * cos_ref[...] + turned_back(value * sin_ref[...])
+        ).astype(BF16)
+
+    loop(2 * inner // 128, unturn)
+    wout_f[...] = dot(att_t[...], gb[...])
+    wout_grad = RowReduce(wout_f, wout_o, wout_x, wout_h, wout_z, o_out, send, recv, 88)
+    qkv_grad = ColumnReduce(qkv_o, qkv_k, qkv_x, qkv_h, qkv_z, send, recv, 96)
+    wout_grad.start()
+    qkv_grad.start(n1t, gpr)
+    gn1_move = SeqReduce(own_gn1, outbox.at[3], inbox.at[3], send, recv, 104)
+    gn1_move.start(gpr, wqkv, NT)
+    gu_grad.relay(0)
+    down_move.finish()
+    wout_grad.relay()
+
+    gu_grad.arrive()
+
+    def gu_sum(rows_now):
+        value = gu_grad.total(rows_now)
+        o_gate[rows_now, pl.ds(gate_start(quarter), whole)] = value[:, :whole]
+        o_up[rows_now, pl.ds(gate_start(quarter), whole)] = value[:, whole : 2 * whole]
+        tail_box[part, rows_now, :] = value[:, 2 * whole :]
+
+    over_rows(gu_grad.rows, 16, gu_sum)
+    shares = [
+        Share(lambda p: o_gate.at[:, pl.ds(gate_start(quarter_of(p)), whole)], send, recv, 108),
+        Share(lambda p: o_up.at[:, pl.ds(gate_start(quarter_of(p)), whole)], send, recv, 111),
+        Share(lambda p: tail_box.at[p], send, recv, 114),
+    ]
+    for share in shares:
+        share.start()
+    for step in range(Z_LEN - 1, -1, -1):
+        qkv_grad.relay(step)
+
+    gn1_move.arrive()
+
+    def first_back(rows_now):
+        here = pl.ds(pl.multiple_of(part * rows + rows_now.start, 16), 16)
+        pulled, summand = rms_back(
+            x_all[here, :].astype(F32), gn1_move.total(rows_now), gain_one
+        )
+        grad_in[rows_now, :] = gmid[rows_now, :] + pulled
+        gain_sum[pl.ds(0, 8), :] += jnp.sum(summand.reshape(2, 8, width), axis=0)
+
+    over_rows(rows, 16, first_back)
+
+    vector[...] = jnp.zeros_like(vector)
+    first_gain = jnp.sum(gain_sum[pl.ds(0, 8), :], axis=0, keepdims=True)
+    second_gain = jnp.sum(gain_sum[pl.ds(8, 8), :], axis=0, keepdims=True)
+    for shard in range(Z_LEN * X_LEN):
+        vector[pl.ds(shard * 8, 1), :] = first_gain[:, shard * 128 : shard * 128 + 128]
+        vector[pl.ds(shard * 8 + 1, 1), :] = second_gain[:, shard * 128 : shard * 128 + 128]
+    for kind in range(3):
+        for piece in range(inner // 128):
+            column = kind * inner + piece * 128
+            row = kind * (width // 128) + quarter * (inner // 128) + piece
+            vector[pl.ds(lax.div(row, 3) * 8 + 2 + lax.rem(row, 3), 1), :] = jnp.sum(
+                gpr[:, column : column + 128].astype(F32), axis=0, keepdims=True
+            )
+    vector_move = VectorReduce(vector, seq_box, dp_box, vec_out, send, recv, 117)
+    vector_move.start()
+    vector_move.relay()
+    wout_grad.finish()
+    qkv_grad.arrive()
+
+    def qkv_spot(p, kind):
+        return pl.ds(pl.multiple_of(kind * width + quarter_of(p) * inner, 128), inner)
+
+    def qkv_sum(rows_now):
+        value = qkv_grad.total(rows_now)
+        for kind in range(3):
+            o_qkv[rows_now, qkv_spot(part, kind)] = value[:, kind * inner : (kind + 1) * inner]
+
+    over_rows(qkv_grad.rows, 16, qkv_sum)
+    for kind in range(3):
+        share = Share(lambda p, kind=kind: o_qkv.at[:, qkv_spot(p, kind)], send, recv, 130 + 3 * kind)
+        share.start()
+        shares.append(share)
+    vector_move.finish()
+    for share in shares:
+        share.finish()
+    low = lanes(rows) < half
+    order = [0, 2, 3, 1]
+    for pair in range(2):
+        even = tail_box[order[2 * pair]].astype(F32)
+        uneven = tail_box[order[2 * pair + 1]].astype(F32)
+        spot = pl.ds(pair * 2 * ff_part + whole, 128)
+        o_gate[:, spot] = jnp.where(low, even, pltpu.roll(uneven, half, axis=1)).astype(BF16)
+        o_up[:, spot] = jnp.where(low, pltpu.roll(even, half, axis=1), uneven).astype(BF16)
+    for move in (
+        x_move, cot_move, small_move, qkv_move, wout_move, gu_move, wdown_move,
+        mid_move, n2_move, gn2_move, out_move, gb_move, gn1_move,
+        down_move, gu_grad, wout_grad, qkv_grad, vector_move,
+    ):
+        move.drain()
+
+
+def ring_body(inputs, gain_attn, w_qkv, b_qkv, w_out, gain_mlp, w_gate, w_up, w_down, cotangent):
+    rows, width = inputs.shape
+    count = Z_LEN * X_LEN
+    inner = HEADS // SEQ_PARTS * HEAD_DIM
+    ff_part = w_gate.shape[1] // SEQ_PARTS
+    padded = (ff_part + 127) // 128 * 128
+    tokens = rows * SEQ_PARTS
+    small = jnp.concatenate(
+        [
+            gain_attn.reshape(1, 128),
+            gain_mlp.reshape(1, 128),
+            b_qkv.reshape(3, 128),
+            jnp.zeros((11, 128), BF16),
+        ]
+    )
+    cosine_tab, sine_tab = rope_tables(jnp.arange(tokens, dtype=jnp.int32))
+    cos_two = jnp.concatenate([cosine_tab, cosine_tab], axis=1)
+    sin_two = jnp.concatenate([sine_tab, sine_tab], axis=1)
+
+    def vm(*shape, dtype=BF16):
+        return pltpu.VMEM(shape, dtype)
+
+    gu_wide, qkv_wide = 2 * ff_part, 3 * inner
+    down_rows, out_rows, shard = w_down.shape[0], w_out.shape[0], w_qkv.shape[0]
+    scratch = [
+        vm(tokens, width), vm(tokens, width), vm(count * 16, 128), vm(count * 16, 128, dtype=F32),
+        vm(8, width, dtype=F32), vm(24, 128, dtype=F32), vm(2, shard, 128),
+        vm(width, qkv_wide), vm(inner, width), vm(width, gu_wide), vm(padded + 64, width),
+        vm(tokens, width), vm(width, tokens), vm(tokens, width), vm(width, tokens),
+        vm(tokens, width), vm(tokens, inner), vm(tokens, inner), vm(tokens, inner),
+        vm(inner, tokens), vm(tokens, inner), vm(inner, tokens),
+        vm(HEADS // SEQ_PARTS, tokens, 128, dtype=F32), vm(rows, width, dtype=F32),
+        vm(tokens, gu_wide, dtype=F32), vm(tokens, padded), vm(padded, tokens),
+        vm(tokens, gu_wide), vm(ff_part, width, dtype=F32), vm(inner, width, dtype=F32),
+        vm(tokens, inner), vm(inner, tokens), vm(tokens, qkv_wide),
+        vm(inner, tokens, dtype=F32), vm(inner, tokens, dtype=F32), vm(rows, width, dtype=F32),
+    ]
+    scratch += [vm(rows, width, dtype=F32)] * 4
+    scratch += [vm(4, SEQ_PARTS - 1, rows, width)] * 2
+    scratch += [vm(down_rows, width)] * 3 + [vm(Z_LEN - 1, down_rows, width)]
+    scratch += [
+        vm(Z_LEN, shard, gu_wide), vm(Z_LEN, shard, gu_wide, dtype=F32), vm(Z_LEN, shard, gu_wide),
+        vm(Z_LEN - 1, shard, gu_wide), vm(Z_LEN - 1, shard, gu_wide),
+    ]
+    scratch += [vm(out_rows, width)] * 3 + [vm(Z_LEN - 1, out_rows, width)]
+    scratch += [
+        vm(Z_LEN, shard, qkv_wide), vm(Z_LEN, shard, qkv_wide, dtype=F32), vm(Z_LEN, shard, qkv_wide),
+        vm(Z_LEN - 1, shard, qkv_wide), vm(Z_LEN - 1, shard, qkv_wide),
+    ]
+    scratch += [
+        vm(SEQ_PARTS, shard, 128), vm(16, width, dtype=F32), vm(count * 8, 128, dtype=F32),
+        vm(SEQ_PARTS, count * 8, 128, dtype=F32), vm(count, 8, 128, dtype=F32),
+        pltpu.SemaphoreType.DMA((140,)), pltpu.SemaphoreType.DMA((140,)),
+        pltpu.SemaphoreType.DMA((16,)),
+    ]
+    output, grad_inputs, sums, g_qkv, g_out, g_gate, g_up, g_down = pl.pallas_call(
+        layer_kernel,
+        out_shape=(
+            jax.ShapeDtypeStruct((rows, width), BF16),
+            jax.ShapeDtypeStruct((rows, width), F32),
+            jax.ShapeDtypeStruct((8, 128), F32),
+            jax.ShapeDtypeStruct(w_qkv.shape, BF16),
+            jax.ShapeDtypeStruct(w_out.shape, BF16),
+            jax.ShapeDtypeStruct(w_gate.shape, BF16),
+            jax.ShapeDtypeStruct(w_up.shape, BF16),
+            jax.ShapeDtypeStruct(w_down.shape, BF16),
+        ),
+        in_specs=[HBM] * 8 + [VMEM] * 2,
+        out_specs=[VMEM] * 8,
+        scratch_shapes=scratch,
+        compiler_params=pltpu.CompilerParams(
+            collective_id=0, has_side_effects=True, vmem_limit_bytes=67043328
+        ),
+    )(inputs, cotangent, small, w_qkv, w_out, w_gate, w_up, w_down, cos_two, sin_two)
+    return (
+        output,
+        grad_inputs,
+        sums[0],
+        g_qkv.astype(F32),
+        sums[2:5].reshape(-1),
+        g_out.astype(F32),
+        sums[1],
+        g_gate.astype(F32),
+        g_up.astype(F32),
+        g_down.astype(F32),
+    )
+
+
 def solution(mesh):
+    tuned = mesh.shape["dp"] == Z_LEN * X_LEN and mesh.shape["seq"] == SEQ_PARTS
     return jax.shard_map(
-        body,
+        ring_body if tuned else generic_body,
         mesh=mesh,
         in_specs=(
             P(("dp", "seq"), None),

time: 1040 us -> 262 us (0.25)
  waiting for transfers between devices: 770 us -> 0 us
  Pallas kernels: 0 us -> 244 us
  blocking collectives: 117 us -> 0 us
  matrix products: 67.6 us -> 0 us
  starting transfers between devices: 26 us -> 0 us
  local copies, waits for them, and re-layouts: 28.5 us -> 4.3 us
  between operations: 16.2 us -> 0.72 us
    reduce_scatter x4 -> x0, waiting for transfers between devices: 423 us -> none  [the longest x1 196 us: body(): lax.psum_scatter(trans_times(columns, gate_up_low).astype(jnp.bfloat16),...]
    all_gather x5 -> x0, waiting for transfers between devices: 308 us -> none  [the longest x1 87.9 us: body(): lax.all_gather(w_gate, 'dp', axis=0, tiled=True)]
    pallas_call x0 -> x1, Pallas kernels: none -> 244 us  [ring_body(): pl.pallas_call(layer_kernel, out_shape=(jax.ShapeDtypeStruct((rows, width...]
    dot_general x20 -> x0, matrix products: 67.6 us -> none  [the longest x5 20.6 us: times_trans(): lax.dot_general(left_op, weight, (((1,), (1,)), ((), ())), preferred_elem...]
    all_gather x3 -> x0, blocking collectives: 67.2 us -> none  [the longest x1 26.6 us: body(): lax.all_gather(b_qkv, 'dp', axis=0, tiled=True)]
    unnamed x1 -> x0, blocking collectives: 34.9 us -> none
    all_to_all x7 -> x0, starting transfers between devices: 25.3 us -> none  [the longest x1 4.26 us: body(): lax.all_to_all(grad_v, 'seq', split_axis=0, concat_axis=1, tiled=True)]
    all_to_all x7 -> x0, waiting for transfers between devices: 20.6 us -> none  [the longest x1 5.95 us: body(): lax.all_to_all(grad_attended.reshape(tokens, HEADS, HEAD_DIM), 'seq', spl...]
  transfers between devices with their start and end apart: 17 -> 0, of which waited for: 13 -> 0; matrix products, arithmetic and copies ran while one was open for 8% -> 0% of each run, Pallas kernels for 0% -> 0%
where the time goes in v2:
time: 262 us; the launch traced here: 259 us
  Pallas kernels  244 us (93%)
  other arithmetic  9.85 us (4%)
  local copies, waits for them, and re-layouts  4.3 us (2%)
    pallas_call x1, Pallas kernels, ring_body(): pl.pallas_call(layer_kernel, out_shape=(jax.ShapeDtypeStruct((rows, width...  244 us

profile of v2, /device:TPU:0, one launch (start us, length us, event | category | flops | bytes accessed | tf_op | source)
XLA Modules:
  0.0 259.1 jit_solution(3423277131041666862)
XLA Ops:
  0.6 0.0 copy-start.8
  0.7 0.0 copy-start.7
  0.7 0.0 copy-start.6
  0.7 1.0 multiply_sine_fusion
  1.7 1.3 pad_maximum_fusion
  3.0 0.1 pad.11.clone
  3.0 0.0 copy-done.8
  3.0 0.0 copy-done.7
  3.0 0.0 copy-done.6
  3.0 0.7 maximum_maximum_fusion.small
  3.7 244.2 %shard_map.177 = (bf16[128,1024]{1,0:T(8,128)(2,1)}, f32[128,1024]{1,0:T(8,128)}, f32[8,128]{1,0:T(8,128)}, bf16[128,3072]{1,0:T(8,128)(2,1)}, bf16[128,1024]{1,...) custom-call(bf16[128,1024]{1,0:T(8,128)(2,1)} %x_in.1, ...), custom_call_target="tpu_custom_call" | custom-call | tf_op jit(solution)/shard_map/pallas_call | solution.py:1330
  247.9 0.0 copy-start.2
  247.9 1.3 slice_bitcast_fusion.1
  249.2 1.3 slice_bitcast_fusion
  250.4 2.4 convert_element_type.59
  252.9 0.0 copy-start.1
  252.9 0.0 copy-done.2
  252.9 1.2 convert_element_type.61
  254.1 0.0 copy-start
  254.1 0.2 copy-done.1
  254.2 1.2 convert_element_type.62
  255.4 0.0 copy-start.4
  255.4 0.0 copy-done
  255.4 0.0 copy-start.5
  255.4 0.0 copy-start.3
  255.5 1.3 convert_element_type.63
  256.7 0.0 copy-done.4
  256.7 0.8 convert_element_type.60
  257.6 0.0 copy-done.5
  257.6 0.7 copy.22
  258.3 0.0 copy-done.3
  258.3 0.8 copy.23
  (3 shorter events, 0.0 us)
Async XLA Ops:
  0.6 2.4 copy-start.8
  0.7 2.4 copy-start.7
  0.7 2.4 copy-start.6
  247.9 5.0 %copy-start.2 = (bf16[128,2816]{1,0:T(8,128)(2,1)S(1)}, bf16[128,2816]{1,0:T(8,128)(2,1)}, u32[]{:S(2)}) copy-start(bf16[128,2816]{1,0:T(8,128)(2,1)} %get-tuple-element.23) | copy-start | bytes 2162692
  252.9 1.4 copy-start.1
  254.1 1.4 copy-start
  255.4 1.3 copy-start.4
  255.4 2.1 copy-start.5
  255.4 2.8 %copy-start.3 = (f32[128,1024]{1,0:T(8,128)S(1)}, f32[128,1024]{1,0:T(8,128)}, u32[]{:S(2)}) copy-start(f32[128,1024]{1,0:T(8,128)} %get-tuple-element.43) | copy-start | bytes 1572868
